TPU v7x, 32 devices: a 4x4x1 block of a 4x4x8 slice. The times are simulated.
32 devices in a mesh: dp: 1 (over z), sp: 32 (over y, x, core).
Axes of the slice: x: 4, y: 4, z: 1, core: 2. Of those that a mesh axis runs over, the one named last changes fastest.
The devices are a block of a 4x4x8 slice.
Arguments:
- x: bfloat16 [16384, 2560], P(('dp', 'sp'))
- doc_start: int32 [16384], P(('dp', 'sp'))
- w_in: bfloat16 [2560, 10576], replicated
- conv_w: float32 [4, 5376], replicated
- conv_b: float32 [5376], replicated
- dt_bias: float32 [80], replicated
- a_log: float32 [80], replicated
- d_skip: float32 [80], replicated
- norm_w: float32 [1, 5120], replicated
- w_out: bfloat16 [5120, 2560], replicated
Outputs:
- output: bfloat16 [16384, 2560], P(('dp', 'sp'))
All inputs are finite; a program needn't handle non-finite values.
Results may differ from a plain program's by a relative error of at most 0.00215957.
Values are sent between devices in bfloat16 or wider.
A program may use at most 768 MiB of HBM per device.

v0:
```python
import math
import jax
import jax.numpy as jnp
from jax import lax
from jax.sharding import PartitionSpec as P

CHUNK_LEN = 256
NORM_EPS = 1e-5


def conv_halo_rows(conv_in, keep_flag, conv_width):
    n_tok = conv_in.shape[0]
    tail_keep = jnp.cumprod(keep_flag[n_tok - conv_width + 2:][::-1])[::-1]
    tail_ok = jnp.concatenate([tail_keep, jnp.ones((1,), jnp.float32)])
    last_rows = conv_in[n_tok - conv_width + 1:]
    return jnp.where(tail_ok[:, None] > 0.5, last_rows, jnp.zeros_like(last_rows))


def causal_conv(conv_in, halo_rows, keep_flag, conv_w, conv_b):
    conv_width = conv_w.shape[0]
    n_tok = conv_in.shape[0]
    ext_rows = jnp.concatenate([halo_rows, conv_in], axis=0)
    keep_ext = jnp.concatenate([jnp.ones((conv_width - 1,), jnp.float32), keep_flag])
    pre_act = conv_b + conv_w[0] * conv_in
    tap_mask = jnp.ones((n_tok,), jnp.float32)
    for offset in range(1, conv_width):
        tap_mask = tap_mask * keep_ext[conv_width - offset:conv_width - offset + n_tok]
        pre_act = pre_act + conv_w[offset] * (tap_mask[:, None] * ext_rows[conv_width - 1 - offset:conv_width - 1 - offset + n_tok])
    return jax.nn.silu(pre_act).astype(jnp.bfloat16)


def local_scan(conv_out, dt_val, doc_start, a_log, groups, d_inner):
    n_tok = conv_out.shape[0]
    n_heads = a_log.shape[0]
    per_group = n_heads // groups
    head_dim = d_inner // n_heads
    state_dim = (conv_out.shape[1] - d_inner) // (2 * groups)
    n_chunks = n_tok // CHUNK_LEN
    xs_chunk = conv_out[:, :d_inner].reshape(n_chunks, CHUNK_LEN, groups, per_group, head_dim)
    b_chunk = conv_out[:, d_inner:d_inner + groups * state_dim].reshape(n_chunks, CHUNK_LEN, groups, state_dim)
    c_chunk = conv_out[:, d_inner + groups * state_dim:].reshape(n_chunks, CHUNK_LEN, groups, state_dim)
    dt_chunk = dt_val.reshape(n_chunks, CHUNK_LEN, groups, per_group)
    cum_decay = jnp.cumsum(-jnp.exp(a_log).reshape(groups, per_group) * dt_chunk, axis=1)
    seg_ids = jnp.cumsum(doc_start.reshape(n_chunks, CHUNK_LEN), axis=1)
    position = jnp.arange(CHUNK_LEN)
    allowed = (position[:, None] >= position[None, :]) & (seg_ids[:, :, None] == seg_ids[:, None, :])
    cum_rows = jnp.moveaxis(cum_decay, 1, -1)
    decay_mat = jnp.exp(jnp.where(allowed[:, None, None], cum_rows[..., :, None] - cum_rows[..., None, :], -jnp.inf))
    scores = jnp.einsum('cign,cjgn->cgij', c_chunk, b_chunk, preferred_element_type=jnp.float32)
    mix_mat = (scores[:, :, None] * decay_mat * jnp.moveaxis(dt_chunk, 1, -1)[..., None, :]).astype(jnp.bfloat16)
    y_intra = jnp.einsum('cgkij,cjgkp->cigkp', mix_mat, xs_chunk, preferred_element_type=jnp.float32)
    last_cum = cum_decay[:, -1]
    end_same = seg_ids == seg_ids[:, -1:]
    w_end = jnp.exp(last_cum[:, None] - cum_decay) * dt_chunk * end_same[..., None, None]
    scaled_x = (xs_chunk * w_end[..., None]).astype(jnp.bfloat16)
    chunk_state = jnp.einsum('cjgkp,cjgn->cgkpn', scaled_x, b_chunk, preferred_element_type=jnp.float32)
    chunk_reset = (seg_ids[:, -1] > 0).astype(jnp.int32)
    chunk_decay = jnp.exp(last_cum) * (chunk_reset == 0)[:, None, None]
    cum_in = jnp.cumsum(last_cum, axis=0)
    cum_ex = cum_in - last_cum
    reset_in = jnp.cumsum(chunk_reset)
    reset_ex = reset_in - chunk_reset
    chunk_idx = jnp.arange(n_chunks)
    link_ok = (chunk_idx[:, None] > chunk_idx[None, :]) & (reset_ex[:, None] == reset_in[None, :])
    carry_w = jnp.exp(jnp.where(link_ok[:, :, None, None], cum_ex[:, None] - cum_in[None, :], -jnp.inf))
    local_start = jnp.einsum('cdgk,dgkpn->cgkpn', carry_w, chunk_state, precision=lax.Precision.HIGHEST)
    start_decay = jnp.exp(cum_ex) * (reset_ex == 0)[:, None, None]
    w_start = jnp.exp(cum_decay) * (seg_ids == 0)[..., None, None]
    return y_intra, local_start, start_decay, w_start, c_chunk, chunk_state, chunk_decay


def finish_layer(y_intra, local_start, start_decay, w_start, c_chunk, state_in, conv_out, gate_in, d_skip, norm_w, w_out):
    n_tok = conv_out.shape[0]
    n_heads = d_skip.shape[0]
    groups, group_width = norm_w.shape
    d_inner = groups * group_width
    head_dim = d_inner // n_heads
    start_states = local_start + start_decay[..., None, None] * state_in
    y_state = jnp.einsum('cign,cgkpn->cigkp', c_chunk, start_states.astype(jnp.bfloat16), preferred_element_type=jnp.float32) * w_start[..., None]
    y_heads = (y_intra + y_state).reshape(n_tok, n_heads, head_dim) + d_skip[:, None] * conv_out[:, :d_inner].reshape(n_tok, n_heads, head_dim)
    gated_y = y_heads.reshape(n_tok, groups, group_width) * jax.nn.silu(gate_in.astype(jnp.float32)).reshape(n_tok, groups, group_width)
    normed = gated_y * lax.rsqrt(jnp.mean(gated_y * gated_y, axis=-1, keepdims=True) + NORM_EPS) * norm_w
    return jnp.dot(normed.reshape(n_tok, d_inner).astype(jnp.bfloat16), w_out, preferred_element_type=jnp.float32).astype(jnp.bfloat16)


def solution(mesh):
    n_seq = mesh.shape['sp']
    n_rounds = int(math.ceil(math.log2(n_seq)))
    next_pairs = [(source, source + 1) for source in range(n_seq - 1)]
    row_spec = P(('dp', 'sp'), None)
    tok_spec = P(('dp', 'sp'))

    def layer_shard(x, doc_start, w_in, conv_w, conv_b, dt_bias, a_log, d_skip, norm_w, w_out):
        groups = norm_w.shape[0]
        d_inner = norm_w.shape[0] * norm_w.shape[1]
        conv_dim = conv_w.shape[1]
        seq_rank = lax.axis_index('sp')
        projected = jnp.dot(x, w_in, preferred_element_type=jnp.float32).astype(jnp.bfloat16)
        conv_in = projected[:, d_inner:d_inner + conv_dim]
        keep_flag = (1 - doc_start).astype(jnp.float32)
        halo_rows = lax.ppermute(conv_halo_rows(conv_in, keep_flag, conv_w.shape[0]), 'sp', next_pairs)
        conv_out = causal_conv(conv_in, halo_rows, keep_flag, conv_w, conv_b)
        dt_val = jax.nn.softplus(projected[:, d_inner + conv_dim:].astype(jnp.float32) + dt_bias)
        pieces = local_scan(conv_out, dt_val, doc_start, a_log, groups, d_inner)
        y_intra, local_start, start_decay, w_start, c_chunk, chunk_state, chunk_decay = pieces
        acc_decay = start_decay[-1] * chunk_decay[-1]
        acc_state = chunk_decay[-1][..., None, None] * local_start[-1] + chunk_state[-1]
        for round_idx in range(n_rounds):
            hop_len = 2 ** round_idx
            hop_pairs = [(source, source + hop_len) for source in range(n_seq - hop_len)]
            got_decay = lax.ppermute(acc_decay, 'sp', hop_pairs)
            got_state = lax.ppermute(acc_state, 'sp', hop_pairs)
            got_decay = jnp.where(seq_rank >= hop_len, got_decay, 1.0)
            acc_state = acc_decay[..., None, None] * got_state + acc_state
            acc_decay = got_decay * acc_decay
        state_in = lax.ppermute(acc_state, 'sp', next_pairs)
        return finish_layer(y_intra, local_start, start_decay, w_start, c_chunk, state_in, conv_out, projected[:, :d_inner], d_skip, norm_w, w_out)

    return jax.shard_map(layer_shard, mesh=mesh, in_specs=(row_spec, tok_spec, P(), P(), P(), P(), P(), P(), P(), P()), out_specs=row_spec, check_vma=False)
```

profile of v0, /device:TPU:97, one launch (start us, length us, event | category | flops | bytes accessed | tf_op | source)
XLA Modules:
  0.0 522.5 jit_solution(1598297211269277925)
XLA Ops:
  0.0 0.8 subtract_convert_fusion
  1.8 37.0 %convolution_convert_fusion = bf16[512,10576]{1,0:T(8,128)(2,1)} fusion(bf16[512,2560]{1,0:T(8,128)(2,1)S(1)} %copy-done, bf16[2560,10576]{0,1:T(8,128)(2,1)} %param.12), kind=kOutput, calls=%fused_computation.8 | convolution fusion | flops 27729764352 | bytes 67600384 | tf_op jit(solution)/shard_map/dot_general | solution.py:98
  38.8 1.0 slice_select_fusion
  39.8 4.8 collective-permute-start
  44.6 1.1 compare_select_fusion
  46.0 1.3 reduce-window.37
  49.8 1.0 exponential_multiply_fusion
  50.7 2.2 slice_reduce_fusion.1
  54.0 5.3 %slice.116 = bf16[512,5376]{1,0:T(8,128)(2,1)} slice(bf16[512,10576]{1,0:T(8,128)(2,1)} %convolution_convert_fusion), slice={[0:512], [5120:10496]} | slice | bytes 11010048 | tf_op jit(solution)/shard_map/slice | solution.py:99
  60.2 17.1 %multiply_convert_fusion.2 = bf16[512,5376]{1,0:T(8,128)(2,1)S(1)} fusion(bf16[512,5376]{1,0:T(8,128)(2,1)} %slice.116, bf16[3,5376]{1,0:T(4,128)(2,1)S(1)} %collective-permute-done, f32[512]{0:T(512)S(1)} %get-tuple-element.13, f32[5376]{0:T(1024)S(1)} %get-tuple-element.7, f32[512]{0:T(512)S(1)} %get-tuple-element.14, f32[5376]{0:T(1024)S(1)} %get-tuple-element.8, ...), kind=kLoop, calls=%fused_computation.11 | loop fusion | flops 79822848 | bytes 11155968 | tf_op jit(solution)/shard_map/convert_element_type | solution.py:29
  77.3 3.4 slice.122
  81.3 8.0 %copy.108 = bf16[512,5120]{0,1:T(8,128)(2,1)} copy(bf16[512,5120]{1,0:T(8,128)(2,1)} %slice.122) | data formatting | bytes 10485760 | tf_op jit(solution)/shard_map/slice | solution.py:39
  89.2 8.3 %reshape.574 = bf16[2,256,80,64]{1,0,3,2:T(2,128)(2,1)} reshape(bf16[512,5120]{0,1:T(8,128)(2,1)} %copy.108) | data formatting | bytes 10485760 | tf_op jit(solution)/shard_map/reshape.37
  97.6 5.3 %multiply_convert_fusion.4 = bf16[2,256,80,64]{1,0,3,2:T(2,128)(2,1)S(1)} fusion(bf16[2,256,80,64]{1,0,3,2:T(2,128)(2,1)} %reshape.574, f32[2,256,80]{1,0,2:T(2,128)S(1)} %bitcast.138), kind=kLoop, calls=%fused_computation.20 | loop fusion | flops 7864320 | bytes 10649600 | tf_op jit(solution)/shard_map/convert_element_type | solution.py:55
  102.9 1.5 fusion.15
  104.4 20.6 %fusion.20 = f32[80,64,128,2]{2,3,1,0:T(2,128)S(1)} fusion(f32[2,80,64,128]{3,2,1,0:T(8,128)S(1)} %fusion.15, pred[2,2]{1,0:T(4,128)(4,1)S(1)} %compare_and_fusion.1, f32[2,80]{0,1:T(8,128)S(1)} %copy.122, f32[2,80]{0,1:T(8,128)S(1)} %bitcast.139), kind=kOutput, calls=%fused_computation.34 | convolution fusion | flops 31457920 | bytes 10487044 | tf_op jit(solution)/shard_map/cdgk,dgkpn->cgkpn/dot_general | solution.py:66
  126.1 1.3 copy-done.2
  127.4 1.9 collective-permute-start.5
  129.3 28.5 %collective-permute-done.5 = f32[1,80,64,128]{3,2,1,0:T(8,128)S(1)} collective-permute-done((f32[1,80,64,128]{3,2,1,0:T(8,128)S(1)}, f32[1,80,64,128]{3,2,1,0:T(8,128)S(1)}, u32[]{:S(2)}, u32[]{:S(2)}) %collective-permute-start.5) | collective-permute-done | bytes 2621472 | tf_op jit(solution)/shard_map/ppermute | solution.py:112
  158.2 4.8 collective-permute-start.6
  163.0 3.2 collective-permute-start.1
  166.2 50.2 %collective-permute-done.1 = f32[1,80]{1,0:T(1,128)S(1)} collective-permute-done((f32[1,80]{1,0:T(1,128)S(1)}, f32[1,80]{1,0:T(1,128)S(1)}, u32[]{:S(2)}, u32[]{:S(2)}) %collective-permute-start.1) | collective-permute-done | bytes 352 | tf_op jit(solution)/shard_map/ppermute | solution.py:111
  216.4 3.5 multiply_add_fusion.3
  220.0 5.5 %collective-permute-start.7 = (f32[1,80,64,128]{3,2,1,0:T(8,128)}, f32[1,80,64,128]{3,2,1,0:T(8,128)S(1)}, u32[]{:S(2)}, u32[]{:S(2)}) collective-permute-start(f32[1,80,64,128]{3,2,1,0:T(8,128)} %multiply_add_fusion.3), channel_id=1, source_target_pairs={{0,4},{1,5},{2,6},{3,7},{4,8},{5,9},{6,10},{7,11},{8,12},{9,13},{1... | collective-permute-start | bytes 7864328 | tf_op jit(solution)/shard_map/ppermute | solution.py:112
  225.5 3.0 collective-permute-start.2
  228.5 50.7 %collective-permute-done.2 = f32[1,80]{1,0:T(1,128)S(1)} collective-permute-done((f32[1,80]{1,0:T(1,128)S(1)}, f32[1,80]{1,0:T(1,128)S(1)}, u32[]{:S(2)}, u32[]{:S(2)}) %collective-permute-start.2) | collective-permute-done | bytes 352 | tf_op jit(solution)/shard_map/ppermute | solution.py:111
  279.2 1.5 copy-done.5
  280.7 2.8 multiply_add_fusion.2
  283.6 5.5 %collective-permute-start.8 = (f32[1,80,64,128]{3,2,1,0:T(8,128)S(1)}, f32[1,80,64,128]{3,2,1,0:T(8,128)}, u32[]{:S(2)}, u32[]{:S(2)}) collective-permute-start(f32[1,80,64,128]{3,2,1,0:T(8,128)S(1)} %multiply_add_fusion.2), channel_id=1, source_target_pairs={{0,8},{1,9},{2,10},{3,11},{4,12},{5,13},{6,14},{7,15},{8,16},{9,17... | collective-permute-start | bytes 7864328 | tf_op jit(solution)/shard_map/ppermute | solution.py:112
  289.1 5.5 %collective-permute-start.3 = (f32[1,80]{1,0:T(1,128)S(1)}, f32[1,80]{1,0:T(1,128)S(1)}, u32[]{:S(2)}, u32[]{:S(2)}) collective-permute-start(f32[1,80]{1,0:T(1,128)S(1)} %fusion.41), channel_id=1, source_target_pairs={{0,4},{1,5},{2,6},{3,7},{4,8},{5,9},{6,10},{7,11},{8,12},{9,13},{1... | collective-permute-start | bytes 968 | tf_op jit(solution)/shard_map/ppermute | solution.py:111
  295.4 42.7 %collective-permute-done.8 = f32[1,80,64,128]{3,2,1,0:T(8,128)} collective-permute-done((f32[1,80,64,128]{3,2,1,0:T(8,128)S(1)}, f32[1,80,64,128]{3,2,1,0:T(8,128)}, u32[]{:S(2)}, u32[]{:S(2)}) %collective-permute-start.8) | collective-permute-done | bytes 2621472 | tf_op jit(solution)/shard_map/ppermute | solution.py:112
  338.1 2.8 multiply_add_fusion.1
  341.0 8.1 %collective-permute-start.9 = (f32[1,80,64,128]{3,2,1,0:T(8,128)S(1)}, f32[1,80,64,128]{3,2,1,0:T(8,128)}, u32[]{:S(2)}, u32[]{:S(2)}) collective-permute-start(f32[1,80,64,128]{3,2,1,0:T(8,128)S(1)} %multiply_add_fusion.1), channel_id=1, source_target_pairs={{0,16},{1,17},{2,18},{3,19},{4,20},{5,21},{6,22},{7,23},{8,24},{9,... | collective-permute-start | bytes 7864328 | tf_op jit(solution)/shard_map/ppermute | solution.py:112
  349.0 0.8 reshape.584
  350.9 0.8 compare_and_fusion
  351.8 2.9 collective-permute-start.4
  354.7 0.9 copy.156
  355.8 1.0 reduce_window_sum.83
  356.8 40.5 %collective-permute-done.4 = f32[1,80]{1,0:T(1,128)S(1)} collective-permute-done((f32[1,80]{1,0:T(1,128)S(1)}, f32[1,80]{1,0:T(1,128)S(1)}, u32[]{:S(2)}, u32[]{:S(2)}) %collective-permute-start.4) | collective-permute-done | bytes 352 | tf_op jit(solution)/shard_map/ppermute | solution.py:111
  397.6 2.2 multiply_add_fusion
  399.8 13.8 %collective-permute-start.10 = (f32[1,80,64,128]{3,2,1,0:T(8,128)S(1)}, f32[1,80,64,128]{3,2,1,0:T(8,128)S(1)}, u32[]{:S(2)}, u32[]{:S(2)}) collective-permute-start(f32[1,80,64,128]{3,2,1,0:T(8,128)S(1)} %multiply_add_fusion), channel_id=1, source_target_pairs={{0,1},{1,2},{2,3},{3,4},{4,5},{5,6},{6,7},{7,8},{8,9},{9,10},{10,1... | collective-permute-start | bytes 7864328 | tf_op jit(solution)/shard_map/ppermute | solution.py:116
  413.7 15.8 %fusion = f32[2,80,64,256]{3,2,1,0:T(8,128)} fusion(f32[2,80,256]{2,1,0:T(8,128)S(1)} %copy-done.6, f32[2,80,256]{2,1,0:T(8,128)S(1)} %reduce_window_sum.83, f32[2,256,256]{2,1,0:T(8,128)S(1)} %fusion.48, pred[2,256,256]{2,1,0:T(8,128)(4,1)S(1)} %copy-done.7, bf16[2,256,80,64]{1,0,3,2:T(2,128)(2,1)} %reshape.574), kind=kOutput, calls=%fused_computation.1 | convolution fusion | flops 1394606080 | bytes 16711680 | tf_op jit(solution)/shard_map/cgkij,cjgkp->cigkp/dot_general | solution.py:51
  429.4 12.8 %collective-permute-done.10 = f32[1,80,64,128]{3,2,1,0:T(8,128)S(1)} collective-permute-done((f32[1,80,64,128]{3,2,1,0:T(8,128)S(1)}, f32[1,80,64,128]{3,2,1,0:T(8,128)S(1)}, u32[]{:S(2)}, u32[]{:S(2)}) %collective-permute-start.10) | collective-permute-done | bytes 2621472 | tf_op jit(solution)/shard_map/ppermute | solution.py:116
  442.2 7.4 %fusion.11 = f32[2,256,1,80,64]{1,4,3,0,2:T(8,128)} fusion(f32[2,80,64,256]{3,2,1,0:T(8,128)} %fusion, f32[2,256,80]{1,2,0:T(8,128)S(1)} %bitcast.136, bf16[2,256,128,1]{2,1,3,0:T(8,128)(2,1)S(1)} %bitcast.133, f32[80,64,128]{2,1,0:T(8,128)S(1)} %bitcast.127, f32[2,80]{1,0:T(2,128)S(1)} %exponential_multiply_fusion.3, f32[80,64,128,2]{2,3,1,0:T(2,128)S(1)} %bitcast.125), kind=kOutput, calls=%fused_computation.17 | convolution fusion | flops 680263680 | bytes 29131392 | tf_op jit(solution)/shard_map/cign,cgkpn->cigkp/dot_general | solution.py:79
  449.5 17.8 %copy.133 = f32[2,256,1,80,64]{4,3,1,0,2:T(8,128)} copy(f32[2,256,1,80,64]{1,4,3,0,2:T(8,128)} %fusion.11) | data formatting | bytes 20971520 | tf_op jit(solution)/shard_map/reshape | solution.py:80
  467.4 17.7 %reshape.592 = f32[512,5120]{1,0:T(8,128)} reshape(f32[2,256,1,80,64]{4,3,1,0,2:T(8,128)} %copy.133) | data formatting | bytes 20971520 | tf_op jit(solution)/shard_map/reshape | solution.py:80
  485.1 14.4 %multiply_reduce_fusion = (f32[512]{0:T(512)S(1)}, f32[512,5120]{1,0:T(8,128)}) fusion(bf16[512,10576]{1,0:T(8,128)(2,1)} %convolution_convert_fusion, f32[512,5120]{1,0:T(8,128)} %reshape.592, bf16[512,5376]{1,0:T(8,128)(2,1)} %copy-done.3, f32[5120]{0:T(1024)S(1)} %mul.435), kind=kLoop, calls=%fused_computation.19 | loop fusion | flops 28835328 | bytes 31479808 | tf_op jit(solution)/shard_map/reduce_sum | solution.py:82
  499.5 23.0 %fusion.22 = bf16[512,2560]{1,0:T(8,128)(2,1)} fusion(bf16[5120,2560]{1,0:T(8,128)(2,1)} %param.19, f32[512,5120]{1,0:T(8,128)} %get-tuple-element.10, f32[5120]{0:T(1024)S(1)} %bitcast.153, f32[512]{0:T(512)S(1)} %add_rsqrt_fusion), kind=kOutput, calls=%fused_computation.36 | convolution fusion | flops 13430947840 | bytes 39344128 | tf_op jit(solution)/shard_map/dot_general | solution.py:83
  (97 shorter events, 9.9 us)
Async XLA Ops:
  0.0 1.8 copy-start
  1.8 42.9 %copy-start.11 = (f32[80]{0:T(128)S(1)}, f32[80]{0:T(128)}, u32[]{:S(2)}) copy-start(f32[80]{0:T(128)} %param.15) | copy-start | bytes 964
  1.8 44.1 %copy-start.14 = (f32[80]{0:T(128)S(1)}, f32[80]{0:T(128)}, u32[]{:S(2)}) copy-start(f32[80]{0:T(128)} %param.16) | copy-start | bytes 964
  1.8 46.1 %copy-start.10 = (s32[512]{0:T(512)S(1)}, s32[512]{0:T(512)}, u32[]{:S(2)}) copy-start(s32[512]{0:T(512)} %param.11) | copy-start | bytes 6148
  1.8 52.0 %copy-start.8 = (f32[4,5376]{1,0:T(4,128)S(1)}, f32[4,5376]{1,0:T(4,128)}, u32[]{:S(2)}) copy-start(f32[4,5376]{1,0:T(4,128)} %param.13) | copy-start | bytes 258052
  39.8 20.4 %collective-permute-start = (bf16[3,5376]{1,0:T(4,128)(2,1)S(1)}, bf16[3,5376]{1,0:T(4,128)(2,1)S(1)}, u32[]{:S(2)}, u32[]{:S(2)}) collective-permute-start(bf16[3,5376]{1,0:T(4,128)(2,1)S(1)} %slice_select_fusion), channel_id=1, source_target_pairs={{0,1},{1,2},{2,3},{3,4},{4,5},{5,6},{6,7},{7,8},{8,9},{9,10},{10,1... | collective-permute-start | bytes 96776 | tf_op jit(solution)/shard_map/ppermute | solution.py:101
  54.0 6.1 %copy-start.9 = (f32[5376]{0:T(1024)S(1)}, f32[5376]{0:T(1024)}, u32[]{:S(2)}) copy-start(f32[5376]{0:T(1024)} %param.14) | copy-start | bytes 64516
  77.3 4.0 copy-start.3
  125.0 2.3 copy-start.2
  127.4 30.5 %collective-permute-start.5 = (f32[1,80,64,128]{3,2,1,0:T(8,128)S(1)}, f32[1,80,64,128]{3,2,1,0:T(8,128)S(1)}, u32[]{:S(2)}, u32[]{:S(2)}) collective-permute-start(f32[1,80,64,128]{3,2,1,0:T(8,128)S(1)} %slice_add_fusion), channel_id=1, source_target_pairs={{0,1},{1,2},{2,3},{3,4},{4,5},{5,6},{6,7},{7,8},{8,9},{9,10},{10,1... | collective-permute-start | bytes 7864328 | tf_op jit(solution)/shard_map/ppermute | solution.py:112
  158.2 58.2 %collective-permute-start.6 = (f32[1,80,64,128]{3,2,1,0:T(8,128)S(1)}, f32[1,80,64,128]{3,2,1,0:T(8,128)}, u32[]{:S(2)}, u32[]{:S(2)}) collective-permute-start(f32[1,80,64,128]{3,2,1,0:T(8,128)S(1)} %multiply_add_fusion.4), channel_id=1, source_target_pairs={{0,2},{1,3},{2,4},{3,5},{4,6},{5,7},{6,8},{7,9},{8,10},{9,11},{10,... | collective-permute-start | bytes 7864328 | tf_op jit(solution)/shard_map/ppermute | solution.py:112
  163.0 53.4 %collective-permute-start.1 = (f32[1,80]{1,0:T(1,128)S(1)}, f32[1,80]{1,0:T(1,128)S(1)}, u32[]{:S(2)}, u32[]{:S(2)}) collective-permute-start(f32[1,80]{1,0:T(1,128)S(1)} %get-tuple-element.19), channel_id=1, source_target_pairs={{0,1},{1,2},{2,3},{3,4},{4,5},{5,6},{6,7},{7,8},{8,9},{9,10},{10,1... | collective-permute-start | bytes 968 | tf_op jit(solution)/shard_map/ppermute | solution.py:111
  220.0 59.2 %collective-permute-start.7 = (f32[1,80,64,128]{3,2,1,0:T(8,128)}, f32[1,80,64,128]{3,2,1,0:T(8,128)S(1)}, u32[]{:S(2)}, u32[]{:S(2)}) collective-permute-start(f32[1,80,64,128]{3,2,1,0:T(8,128)} %multiply_add_fusion.3), channel_id=1, source_target_pairs={{0,4},{1,5},{2,6},{3,7},{4,8},{5,9},{6,10},{7,11},{8,12},{9,13},{1... | collective-permute-start | bytes 7864328 | tf_op jit(solution)/shard_map/ppermute | solution.py:112
  225.5 53.7 %collective-permute-start.2 = (f32[1,80]{1,0:T(1,128)S(1)}, f32[1,80]{1,0:T(1,128)S(1)}, u32[]{:S(2)}, u32[]{:S(2)}) collective-permute-start(f32[1,80]{1,0:T(1,128)S(1)} %fusion.42), channel_id=1, source_target_pairs={{0,2},{1,3},{2,4},{3,5},{4,6},{5,7},{6,8},{7,9},{8,10},{9,11},{10,... | collective-permute-start | bytes 968 | tf_op jit(solution)/shard_map/ppermute | solution.py:111
  279.2 1.5 copy-start.5
  283.6 54.5 %copy-start.4 = (f32[1,80,64,128]{3,2,1,0:T(8,128)}, f32[1,80,64,128]{3,2,1,0:T(8,128)S(1)}, u32[]{:S(2)}) copy-start(f32[1,80,64,128]{3,2,1,0:T(8,128)S(1)} %multiply_add_fusion.2) | copy-start | bytes 7864324
  283.6 72.0 %copy-start.12 = (f32[80]{0:T(128)S(1)}, f32[80]{0:T(128)}, u32[]{:S(2)}) copy-start(f32[80]{0:T(128)} %param.17) | copy-start | bytes 964
  283.6 54.5 %collective-permute-start.8 = (f32[1,80,64,128]{3,2,1,0:T(8,128)S(1)}, f32[1,80,64,128]{3,2,1,0:T(8,128)}, u32[]{:S(2)}, u32[]{:S(2)}) collective-permute-start(f32[1,80,64,128]{3,2,1,0:T(8,128)S(1)} %multiply_add_fusion.2), channel_id=1, source_target_pairs={{0,8},{1,9},{2,10},{3,11},{4,12},{5,13},{6,14},{7,15},{8,16},{9,17... | collective-permute-start | bytes 7864328 | tf_op jit(solution)/shard_map/ppermute | solution.py:112
  289.1 6.2 %collective-permute-start.3 = (f32[1,80]{1,0:T(1,128)S(1)}, f32[1,80]{1,0:T(1,128)S(1)}, u32[]{:S(2)}, u32[]{:S(2)}) collective-permute-start(f32[1,80]{1,0:T(1,128)S(1)} %fusion.41), channel_id=1, source_target_pairs={{0,4},{1,5},{2,6},{3,7},{4,8},{5,9},{6,10},{7,11},{8,12},{9,13},{1... | collective-permute-start | bytes 968 | tf_op jit(solution)/shard_map/ppermute | solution.py:111
  341.0 56.6 %collective-permute-start.9 = (f32[1,80,64,128]{3,2,1,0:T(8,128)S(1)}, f32[1,80,64,128]{3,2,1,0:T(8,128)}, u32[]{:S(2)}, u32[]{:S(2)}) collective-permute-start(f32[1,80,64,128]{3,2,1,0:T(8,128)S(1)} %multiply_add_fusion.1), channel_id=1, source_target_pairs={{0,16},{1,17},{2,18},{3,19},{4,20},{5,21},{6,22},{7,23},{8,24},{9,... | collective-permute-start | bytes 7864328 | tf_op jit(solution)/shard_map/ppermute | solution.py:112
  351.8 61.9 %copy-start.6 = (f32[2,80,256]{2,1,0:T(8,128)S(1)}, f32[2,80,256]{2,1,0:T(8,128)}, u32[]{:S(2)}) copy-start(f32[2,80,256]{2,1,0:T(8,128)} %copy.113) | copy-start | bytes 491524
  351.8 45.5 %collective-permute-start.4 = (f32[1,80]{1,0:T(1,128)S(1)}, f32[1,80]{1,0:T(1,128)S(1)}, u32[]{:S(2)}, u32[]{:S(2)}) collective-permute-start(f32[1,80]{1,0:T(1,128)S(1)} %fusion.40), channel_id=1, source_target_pairs={{0,8},{1,9},{2,10},{3,11},{4,12},{5,13},{6,14},{7,15},{8,16},{9,17... | collective-permute-start | bytes 968 | tf_op jit(solution)/shard_map/ppermute | solution.py:111
  355.8 57.9 %copy-start.7 = (pred[2,256,256]{2,1,0:T(8,128)(4,1)S(1)}, pred[2,256,256]{2,1,0:T(8,128)(4,1)}, u32[]{:S(2)}) copy-start(pred[2,256,256]{2,1,0:T(8,128)(4,1)} %compare_and_fusion) | copy-start | bytes 393220
  397.5 44.6 %slice-start = ((s8[5242880]{0:T(1024)(128)(4,1)}), s8[4194304]{0:T(1024)(128)(4,1)S(1)}, s32[]{:S(2)}) async-start(s8[5242880]{0:T(1024)(128)(4,1)} %bitcast.124), calls=%async_computation | async-start | bytes 8388608
  399.8 42.4 %slice-start.1 = ((s8[5242880]{0:T(1024)(128)(4,1)}), s8[1048576]{0:T(1024)(128)(4,1)S(1)}, s32[]{:S(2)}) async-start(s8[5242880]{0:T(1024)(128)(4,1)} %bitcast.124), calls=%async_computation.1 | async-start | bytes 2097152
  399.8 42.4 %collective-permute-start.10 = (f32[1,80,64,128]{3,2,1,0:T(8,128)S(1)}, f32[1,80,64,128]{3,2,1,0:T(8,128)S(1)}, u32[]{:S(2)}, u32[]{:S(2)}) collective-permute-start(f32[1,80,64,128]{3,2,1,0:T(8,128)S(1)} %multiply_add_fusion), channel_id=1, source_target_pairs={{0,1},{1,2},{2,3},{3,4},{4,5},{5,6},{6,7},{7,8},{8,9},{9,10},{10,1... | collective-permute-start | bytes 7864328 | tf_op jit(solution)/shard_map/ppermute | solution.py:116
  485.1 14.4 %copy-start.13 = (f32[1,5120]{1,0:T(1,128)S(1)}, f32[1,5120]{1,0:T(1,128)}, u32[]{:S(2)}) copy-start(f32[1,5120]{1,0:T(1,128)} %param.18) | copy-start | bytes 61444
  499.5 23.1 %copy-start.1 = (bf16[512,2560]{1,0:T(8,128)(2,1)S(1)}, bf16[512,2560]{1,0:T(8,128)(2,1)}, u32[]{:S(2)}) copy-start(bf16[512,2560]{1,0:T(8,128)(2,1)} %param.10) | copy-start | bytes 7864324
where the time goes:
time: 524 us; the launch traced here: 523 us
  waiting for transfers between devices  226 us (43%)
  matrix products  105 us (20%)
  local copies, waits for them, and re-layouts  73 us (14%)
  starting transfers between devices  59.1 us (11%)
  other arithmetic  58.3 us (11%)
    ppermute x4, waiting for transfers between devices, layer_shard(): got_decay = lax.ppermute(acc_decay, 'sp', hop_pairs)  142 us
    ppermute x5, waiting for transfers between devices, layer_shard(): got_state = lax.ppermute(acc_state, 'sp', hop_pairs)  71.3 us
    dot_general x1, matrix products, layer_shard(): jnp.dot(x, w_in, preferred_element_type=jnp.float32).astype(jnp.bfloat16)  37 us
    reshape x2, local copies, waits for them, and re-layouts, finish_layer(): (y_intra + y_state).reshape(n_tok, n_heads, head_dim)  35.5 us
    ppermute x5, starting transfers between devices, layer_shard(): got_state = lax.ppermute(acc_state, 'sp', hop_pairs)  25.8 us
    dot_general x1, matrix products, finish_layer(): jnp.dot(normed.reshape(n_tok, d_inner).astype(jnp.bfloat16), w_out, prefe...  23 us
    dot_general x1, matrix products, local_scan(): jnp.einsum('cdgk,dgkpn->cgkpn', carry_w, chunk_state, precision=lax.Preci...  20.6 us
    convert_element_type x1, other arithmetic, causal_conv(): return jax.nn.silu(pre_act).astype(jnp.bfloat16)  17.1 us
  transfers between devices with their start and end apart: 11, of which 7 were waited for; matrix products, arithmetic and copies ran while one was open for 7% of the time, Pallas kernels for 0%

commit v1 on v0

v1 whole, which is shorter than its diff:
```python
import functools
import math

import jax
import jax.numpy as jnp
from jax import lax
from jax.experimental import pallas as pl
from jax.experimental.pallas import tpu as pltpu
from jax.sharding import PartitionSpec as P

CHUNK = 256
HALF = 128
EPS = 1e-5
LB = 512
LANES = 128
HALO = 16
ROWS = 64
LOG2E = math.log2(math.e)
MESH = pl.DeviceIdType.MESH
F32 = jnp.float32
BF16 = jnp.bfloat16


def dot(a, b):
    return jnp.dot(a, b, preferred_element_type=F32)


def dot_nt(a, b):
    return lax.dot_general(a, b, (((1,), (1,)), ((), ())), preferred_element_type=F32)


def split3(v):
    s1 = v.astype(BF16)
    r1 = v - s1.astype(F32)
    s2 = r1.astype(BF16)
    s3 = (r1 - s2.astype(F32)).astype(BF16)
    return s1, s2, s3


def half_silu(c):
    return c + c * jnp.tanh(c)


def mixer_kernel(dims, x_hbm, ds_ref, w_hbm, wdt_ref, cw_ref, cb_ref, dtb_ref, alog_ref, dsk_ref, nw_ref, g_hbm,
                 xe, wbuf, wbcd, zb, xb, yb, us, sc, cs0, tsend, two, tc, hrecv, hout, s0r, fbuf, soth,
                 bc, bt, gm, a2, apt, ldt, we, ws, arl, prm, dec, dpair, dchip, dg, mk, ssq, hal,
                 xsem, wsem, bsem, hs_sem, hr_sem, dp_sem, dps_sem, dg_sem, dgs_sem,
                 ps_sem, pr_sem, s1_sem, r1_sem, s2_sem, r2_sem, fs_sem, fr_sem, gsem):
    n_seq, n_tok, d_model, d_inner, n_heads, state_dim = dims
    head_dim = d_inner // n_heads
    nb = d_inner // LB
    hb = LB // head_dim
    npair = nb // 2
    n_chip = n_seq // 2
    hrows = state_dim // n_chip
    n_lt = LB // LANES
    n_zfirst = 2

    me = lax.axis_index('sp')
    chip = me // 2
    core = lax.rem(me, 2)
    partner = chip * 2 + (1 - core)

    def dev(i):
        return {'sp': i}

    def wcol(t):
        i2 = t - n_zfirst
        pair = i2 // 2
        own = lax.rem(i2, 2)
        ub = 2 * pair + jnp.where(own == 0, 1 - core, core)
        col = jnp.where(t < n_zfirst, t * LB,
                        jnp.where(t < n_zfirst + nb, d_inner + ub * LB, (t - nb) * LB))
        return pl.multiple_of(col, LB)

    def wcopy(t):
        slot = lax.rem(t, 3)
        return pltpu.make_async_copy(w_hbm.at[:, pl.ds(wcol(t), LB)], wbuf.at[slot], wsem.at[slot])

    n_steps = 2 * nb

    def wnext(t):
        wcopy(t).wait()

        @pl.when(t + 2 < n_steps)
        def _():
            wcopy(t + 2).start()

    xcopy = pltpu.make_async_copy(x_hbm, xe.at[pl.ds(HALO, n_tok)], xsem)
    xcopy.start()
    wcopy(jnp.int32(0)).start()
    bcopy = pltpu.make_async_copy(w_hbm.at[:, pl.ds(2 * d_inner, 2 * state_dim)], wbcd, bsem)
    bcopy.start()
    wcopy(jnp.int32(1)).start()

    barrier = pltpu.get_barrier_semaphore()
    pl.semaphore_signal(barrier, inc=1, device_id=dev(lax.rem(me + 1, n_seq)), device_id_type=MESH)
    pl.semaphore_signal(barrier, inc=1, device_id=dev(lax.rem(me + n_seq - 1, n_seq)), device_id_type=MESH)

    @pl.loop(1, n_chip)
    def _(r):
        pl.semaphore_signal(barrier, inc=1, device_id=dev(lax.rem(me + 2 * r, n_seq)), device_id_type=MESH)

    ri = lax.broadcasted_iota(jnp.int32, (CHUNK, CHUNK), 0)
    ci = lax.broadcasted_iota(jnp.int32, (CHUNK, CHUNK), 1)
    tri = (ri >= ci).astype(F32).astype(BF16)
    eye = (ri == ci).astype(F32).astype(BF16)
    n_chunks = n_tok // CHUNK
    per = CHUNK // LANES
    seg_cols, seg_rows, ds_cols = [], [], []
    for c in range(n_chunks):
        row = jnp.concatenate([ds_ref[per * c + q:per * c + q + 1, :] for q in range(per)], axis=1).astype(F32)
        row = jnp.broadcast_to(row, (8, CHUNK)).astype(BF16)
        ds_cols.append(jnp.broadcast_to(dot_nt(eye, row)[:, 0:1], (CHUNK, LANES)))
        seg_cols.append(jnp.broadcast_to(dot_nt(tri, row)[:, 0:1], (CHUNK, LANES)))
        seg_rows.append(dot_nt(row, tri)[0:1, :])
    keep = 1.0 - jnp.concatenate(ds_cols, axis=0)
    tok = lax.broadcasted_iota(jnp.int32, (n_tok, LANES), 0)
    m1 = keep
    k1 = jnp.where(tok >= 1, pltpu.roll(keep, 1, 0), 1.0)
    k2 = jnp.where(tok >= 2, pltpu.roll(keep, 2, 0), 1.0)
    mk[0] = m1
    mk[1] = m1 * k1
    mk[2] = m1 * k1 * k2

    xcopy.wait()
    hrow = lax.broadcasted_iota(jnp.int32, (HALO, LANES), 0)
    k_last = jnp.broadcast_to(mk[0, n_tok - 8:n_tok, :][7:8, :], (HALO, LANES))
    k_last2 = jnp.broadcast_to(mk[1, n_tok - 8:n_tok, :][7:8, :], (HALO, LANES))
    hmask = jnp.where(hrow == HALO - 1, 1.0, jnp.where(hrow == HALO - 2, k_last, jnp.where(hrow == HALO - 3, k_last2, 0.0)))
    for q in range(d_model // LANES):
        hal[:, q * LANES:(q + 1) * LANES] = (xe[n_tok:n_tok + HALO, q * LANES:(q + 1) * LANES].astype(F32) * hmask).astype(BF16)

    def zblock(t, zi):
        wnext(t)
        slot = lax.rem(t, 3)
        for q in range(n_tok // CHUNK):
            zb[zi, q * CHUNK:(q + 1) * CHUNK] = dot(xe[HALO + q * CHUNK:HALO + (q + 1) * CHUNK], wbuf[slot]).astype(BF16)

    pl.semaphore_wait(barrier, n_chip + 1)
    halo_send = pltpu.make_async_remote_copy(
        src_ref=hal, dst_ref=xe.at[pl.ds(0, HALO)], send_sem=hs_sem, recv_sem=hr_sem,
        device_id=dev(lax.rem(me + 1, n_seq)), device_id_type=MESH)

    @pl.when(me < n_seq - 1)
    def _():
        halo_send.start()

    @pl.when(me == 0)
    def _():
        xe[0:HALO, :] = jnp.zeros((HALO, d_model), BF16)

    @pl.loop(0, n_zfirst)
    def _(t):
        zblock(t, t)

    @pl.when(me > 0)
    def _():
        halo_send.wait_recv()

    bcopy.wait()
    mrow = (n_tok + HALO) // 3
    lane = lax.broadcasted_iota(jnp.int32, (1, LANES), 1)
    for q in range(3):
        us[q * mrow:(q + 1) * mrow, 0:2 * state_dim] = dot(xe[q * mrow:(q + 1) * mrow], wbcd[...]).astype(BF16).astype(F32)
        us[q * mrow:(q + 1) * mrow, 2 * state_dim:2 * state_dim + LANES] = dot(xe[q * mrow:(q + 1) * mrow], wdt_ref[...]).astype(BF16).astype(F32)

    def conv(r0, lt, wl):
        cols = slice(lt * LANES, (lt + 1) * LANES)
        ext = us[pl.ds(pl.multiple_of(r0 + HALO - 8, 8), ROWS + 8), cols]
        wl = pl.multiple_of(wl, LANES)
        cw = cw_ref[:, pl.ds(wl, LANES)] * 0.5
        v = cb_ref[:, pl.ds(wl, LANES)] * 0.5 + cw[0:1] * ext[8:8 + ROWS]
        for k in range(1, 4):
            v = v + cw[k:k + 1] * (mk[k - 1, pl.ds(r0, ROWS), :] * ext[8 - k:8 - k + ROWS])
        return half_silu(v)

    @pl.loop(0, n_tok // ROWS)
    def _(q):
        r0 = pl.multiple_of(q * ROWS, ROWS)
        for lt in range(2 * state_dim // LANES):
            bc[pl.ds(r0, ROWS), lt * LANES:(lt + 1) * LANES] = conv(r0, lt, d_inner + lt * LANES).astype(BF16)

    prm[...] = jnp.zeros((8, LANES), F32)
    prm[0:1, 0:n_heads] = dtb_ref[...]
    prm[1:2, 0:n_heads] = alog_ref[...]
    prm[2:3, 0:n_heads] = dsk_ref[...]
    pv = prm[...]
    head_ok = lane < n_heads
    neg_a = jnp.where(head_ok, -jnp.exp(pv[1:2]) , 0.0)
    e_rows = []
    for c in range(n_chunks):
        rows = slice(c * CHUNK, (c + 1) * CHUNK)
        raw = jnp.where(head_ok, us[HALO + c * CHUNK:HALO + (c + 1) * CHUNK, 2 * state_dim:2 * state_dim + LANES], 0.0) + pv[0:1]
        dt = jnp.maximum(raw, 0.0) + jnp.log1p(jnp.exp(-jnp.abs(raw)))
        s1, s2, s3 = split3(neg_a * dt * LOG2E)
        acum = dot(tri, s3) + dot(tri, s2) + dot(tri, s1)
        a2[rows, :] = acum
        a_t = jnp.transpose(acum)
        ld_t = jnp.transpose(jnp.log2(dt))
        ldt[:, rows] = ld_t
        apt[:, rows] = a_t - ld_t
        seg = seg_cols[c]
        last = acum[CHUNK - 1:CHUNK, :]
        seg_last = seg[CHUNK - 1:CHUNK, :]
        ws[rows, :] = jnp.where(seg == 0.0, jnp.exp2(acum), 0.0)
        we[rows, :] = jnp.where(seg == seg_last, jnp.exp2(last - acum) * dt, 0.0)
        e_rows.append(jnp.where(seg_last == 0.0, jnp.exp2(last), 0.0))
        b_c = bc[rows, 0:state_dim]
        c_c = bc[rows, state_dim:2 * state_dim]
        b_t = jnp.transpose(b_c.astype(F32)).astype(BF16)
        bt[c] = b_t
        scores = dot(c_c, b_t)
        same = jnp.concatenate([seg] * per, axis=1) == seg_rows[c]
        gm[c] = jnp.where(jnp.logical_and(ri >= ci, same), scores, 0.0)
    d_own = e_rows[0] * e_rows[1]
    dec[0:1, :] = e_rows[0]
    dec[1:2, :] = e_rows[1]
    dpair[core] = jnp.broadcast_to(d_own, (8, LANES))

    pair_send = pltpu.make_async_remote_copy(
        src_ref=dpair.at[core], dst_ref=dpair.at[core], send_sem=dps_sem, recv_sem=dp_sem,
        device_id=dev(partner), device_id_type=MESH)
    pair_send.start()
    pair_send.wait()
    dchip[...] = dpair[0] * dpair[1]
    dg[chip] = dpair[0] * dpair[1]
    dec[2:3, :] = dpair[0][0:1]
    dec[3:4, :] = dpair[1][0:1]

    @pl.loop(1, n_chip)
    def _(r):
        q = lax.rem(chip + r, n_chip)
        pltpu.make_async_remote_copy(
            src_ref=dchip, dst_ref=dg.at[chip], send_sem=dgs_sem, recv_sem=dg_sem,
            device_id=dev(2 * q + core), device_id_type=MESH).start()

    def expand(v, b):
        n = v.shape[0]
        r = pltpu.roll(v, lax.rem(2 * LANES - hb * b, LANES), 1)
        low = lax.broadcasted_iota(jnp.int32, (n, LANES), 1) < head_dim
        out = []
        for p in range(n_lt):
            out.append(jnp.where(low, jnp.broadcast_to(r[:, 2 * p:2 * p + 1], (n, LANES)),
                                 jnp.broadcast_to(r[:, 2 * p + 1:2 * p + 2], (n, LANES))))
        return jnp.concatenate(out, axis=1)

    def roll_to(dst, src, b):
        sh = lax.rem(2 * LANES - hb * b, LANES)
        for q in range(n_tok // LANES):
            dst[q * LANES:(q + 1) * LANES, :] = pltpu.roll(src[q * LANES:(q + 1) * LANES, :], sh, 1)

    low_r = lax.broadcasted_iota(jnp.int32, (ROWS, LANES), 1) < head_dim

    def head_cols(r0, lt):
        wv = arl[pl.ds(r0, ROWS), :]
        return jnp.where(low_r, jnp.broadcast_to(wv[:, 2 * lt:2 * lt + 1], (ROWS, LANES)),
                         jnp.broadcast_to(wv[:, 2 * lt + 1:2 * lt + 2], (ROWS, LANES)))

    def ublock(t, b, t_ref):
        wnext(t)
        slot = lax.rem(t, 3)
        for q in range(3):
            us[q * mrow:(q + 1) * mrow, :] = dot(xe[q * mrow:(q + 1) * mrow], wbuf[slot]).astype(BF16).astype(F32)
        roll_to(arl, we, b)

        @pl.loop(0, n_tok // ROWS)
        def _(q):
            r0 = pl.multiple_of(q * ROWS, ROWS)
            for lt in range(n_lt):
                cols = slice(lt * LANES, (lt + 1) * LANES)
                xs = conv(r0, lt, b * LB + lt * LANES).astype(BF16)
                xb[b, pl.ds(r0, ROWS), cols] = xs
                sc[pl.ds(r0, ROWS), cols] = (xs.astype(F32) * head_cols(r0, lt)).astype(BF16)

        ex = expand(dec[...], b)
        st0 = dot(bt[0], sc[0:CHUNK])
        cs0[b] = st0
        t_ref[...] = ex[1:2] * st0 + dot(bt[1], sc[CHUNK:2 * CHUNK])

    def part_copy(i):
        return pltpu.make_async_remote_copy(
            src_ref=tsend.at[i], dst_ref=two.at[i, core], send_sem=ps_sem.at[i], recv_sem=pr_sem.at[i],
            device_id=dev(partner), device_id_type=MESH)

    def home_copy(i, q):
        return pltpu.make_async_remote_copy(
            src_ref=tc.at[i, q], dst_ref=hrecv.at[i, chip], send_sem=s1_sem.at[i], recv_sem=r1_sem.at[i],
            device_id=dev(2 * q + core), device_id_type=MESH)

    def back_copy(i, q):
        return pltpu.make_async_remote_copy(
            src_ref=hout.at[i, q], dst_ref=s0r.at[i, chip], send_sem=s2_sem.at[i], recv_sem=r2_sem.at[i],
            device_id=dev(2 * q + core), device_id_type=MESH)

    def all_copies(src, dst, send_sem, recv_sem):
        return pltpu.make_async_remote_copy(
            src_ref=src.at[pl.ds(0, n_chip - 1)], dst_ref=dst.at[pl.ds(0, n_chip - 1)], send_sem=send_sem, recv_sem=recv_sem,
            device_id=dev(partner), device_id_type=MESH)

    def fin_copy(i):
        return pltpu.make_async_remote_copy(
            src_ref=fbuf.at[i, 1 - core], dst_ref=soth.at[i], send_sem=fs_sem.at[i], recv_sem=fr_sem.at[i],
            device_id=dev(partner), device_id_type=MESH)

    def send_home(i, b):
        part_copy(i).wait_recv()
        ex = expand(dec[...], b)
        for q in range(n_chip):
            rows = slice(q * hrows, (q + 1) * hrows)
            tc[i, q] = ex[3:4] * two[i, 0, rows] + two[i, 1, rows]
        hrecv[i, chip] = tc[i, chip]

        @pl.loop(1, n_chip)
        def _(r):
            home_copy(i, lax.rem(chip + r, n_chip)).start()

    def home(i):
        b = 2 * i + core
        all_copies(tc.at[i], hrecv.at[i], s1_sem.at[i], r1_sem.at[i]).wait_recv()
        run = jnp.zeros((hrows, LB), F32)
        for q in range(n_chip):
            hout[i, q] = run
            run = expand(dg[q], b)[0:1] * run + hrecv[i, q]
        s0r[i, chip] = hout[i, chip]

        @pl.loop(1, n_chip)
        def _(r):
            back_copy(i, lax.rem(chip + r, n_chip)).start()

    def finish(i):
        b = 2 * i + core
        all_copies(hout.at[i], s0r.at[i], s2_sem.at[i], r2_sem.at[i]).wait_recv()
        ex = expand(dec[...], b)
        for q in range(n_chip):
            rows = slice(q * hrows, (q + 1) * hrows)
            fbuf[i, 0, rows] = s0r[i, q]
            fbuf[i, 1, rows] = ex[2:3] * s0r[i, q] + two[i, 0, rows]
        fin_copy(i).start()

    @pl.loop(0, npair)
    def _(i):
        t = n_zfirst + 2 * i
        ublock(t, 2 * i + 1 - core, tsend.at[i])
        part_copy(i).start()
        ublock(t + 1, 2 * i + core, two.at[i, core])
        send_home(i, 2 * i + core)

        @pl.when(i == 0)
        def _():
            all_copies(dg, dg, dgs_sem, dg_sem).wait_recv()

        @pl.when(i >= 1)
        def _():
            home(i - 1)

        @pl.when(i >= 2)
        def _():
            finish(i - 2)

    low_b = (lax.broadcasted_iota(jnp.int32, (CHUNK, LANES), 1) < head_dim).astype(F32).astype(BF16)
    high_b = (lax.broadcasted_iota(jnp.int32, (CHUNK, LANES), 1) >= head_dim).astype(F32).astype(BF16)

    def intra(b):
        roll_to(arl, a2, b)
        hrows8 = pl.ds(pl.multiple_of(b * hb, hb), hb)
        dsk = expand(prm[...], b)[2:3]
        for c in range(n_chunks):
            r0 = c * CHUNK
            for p in range(n_lt):
                cols = slice(p * LANES, (p + 1) * LANES)
                lhs0, lhs1 = [], []
                for h in (2 * p, 2 * p + 1):
                    ai0 = jnp.broadcast_to(arl[r0:r0 + HALF, h:h + 1], (HALF, HALF))
                    ai1 = jnp.broadcast_to(arl[r0 + HALF:r0 + CHUNK, h:h + 1], (HALF, HALF))
                    aj = apt[hrows8, r0:r0 + CHUNK][h:h + 1]
                    ld = ldt[hrows8, r0:r0 + CHUNK][h:h + 1]
                    lhs0.append((jnp.exp2(jnp.minimum(ai0 - aj[:, :HALF], ld[:, :HALF])) * gm[c, 0:HALF, 0:HALF]).astype(BF16))
                    lhs1.append((jnp.exp2(ai1 - aj[:, :HALF]) * gm[c, HALF:CHUNK, 0:HALF]).astype(BF16))
                    lhs1.append((jnp.exp2(jnp.minimum(ai1 - aj[:, HALF:], ld[:, HALF:])) * gm[c, HALF:CHUNK, HALF:CHUNK]).astype(BF16))
                xp = xb[b, r0:r0 + CHUNK, cols]
                xa, xh = xp * low_b, xp * high_b
                y0 = dot(jnp.concatenate(lhs0, axis=1), jnp.concatenate([xa[:HALF], xh[:HALF]], axis=0))
                y1 = dot(jnp.concatenate(lhs1, axis=1), jnp.concatenate([xa, xh], axis=0))
                yb[b, r0:r0 + HALF, cols] = y0 + dsk[:, cols] * xp[:HALF].astype(F32)
                yb[b, r0 + HALF:r0 + CHUNK, cols] = y1 + dsk[:, cols] * xp[HALF:].astype(F32)

    @pl.loop(0, nb)
    def _(m):
        intra(m)

        @pl.when(m < nb - n_zfirst)
        def _():
            zblock(m + n_zfirst + nb, m + n_zfirst)

        @pl.when(m == 0)
        def _():
            home(npair - 1)

        @pl.when(m == 1)
        def _():
            finish(npair - 2)

        @pl.when(m == nb - 5)
        def _():
            finish(npair - 1)

    ssq[...] = jnp.zeros((n_tok, LANES), F32)

    def close(b, s_ref):
        ex = expand(dec[...], b)
        roll_to(arl, ws, b)
        s_in = s_ref[...]
        us[0:CHUNK, :] = dot(bc[0:CHUNK, state_dim:2 * state_dim], s_in.astype(BF16))
        s_mid = ex[0:1] * s_in + cs0[b]
        us[CHUNK:2 * CHUNK, :] = dot(bc[CHUNK:2 * CHUNK, state_dim:2 * state_dim], s_mid.astype(BF16))

        @pl.loop(0, n_tok // ROWS)
        def _(q):
            rows = pl.ds(pl.multiple_of(q * ROWS, ROWS), ROWS)
            acc = ssq[rows, :]
            for lt in range(n_lt):
                cols = slice(lt * LANES, (lt + 1) * LANES)
                y = yb[b, rows, cols] + head_cols(q * ROWS, lt) * us[rows, cols]
                gated = y * half_silu(zb[b, rows, cols].astype(F32) * 0.5)
                yb[b, rows, cols] = gated
                acc = acc + gated * gated
            ssq[rows, :] = acc

    @pl.loop(0, npair)
    def _(i):
        close(2 * i + core, fbuf.at[i, core])
        fin_copy(i).wait_recv()
        close(2 * i + 1 - core, soth.at[i])

    scale = lax.rsqrt(jnp.sum(ssq[...], axis=1, keepdims=True) * (1.0 / d_inner) + EPS)
    ssq[...] = jnp.broadcast_to(scale, (n_tok, LANES))

    def gcopy(b):
        return pltpu.make_async_copy(zb.at[b], g_hbm.at[:, pl.ds(pl.multiple_of(b * LB, LB), LB)], gsem.at[b])

    @pl.loop(0, nb)
    def _(b):
        @pl.loop(0, n_tok // ROWS)
        def _(q):
            rows = pl.ds(pl.multiple_of(q * ROWS, ROWS), ROWS)
            sv = ssq[rows, :]
            for lt in range(n_lt):
                cols = slice(lt * LANES, (lt + 1) * LANES)
                nw = nw_ref[:, pl.ds(pl.multiple_of(b * LB + lt * LANES, LANES), LANES)]
                zb[b, rows, cols] = (yb[b, rows, cols] * sv * nw).astype(BF16)
        gcopy(b).start()

    @pl.when(me < n_seq - 1)
    def _():
        halo_send.wait_send()

    all_copies(dg, dg, dgs_sem, dg_sem).wait_send()

    @pl.loop(0, npair)
    def _(i):
        part_copy(i).wait_send()
        all_copies(tc.at[i], hrecv.at[i], s1_sem.at[i], r1_sem.at[i]).wait_send()
        all_copies(hout.at[i], s0r.at[i], s2_sem.at[i], r2_sem.at[i]).wait_send()
        fin_copy(i).wait_send()

    @pl.loop(0, nb)
    def _(b):
        gcopy(b).wait()


def mixer(n_seq, x, doc_start, w_in, conv_w, conv_b, dt_bias, a_log, d_skip, norm_w):
    n_tok, d_model = x.shape
    d_inner = norm_w.shape[0] * norm_w.shape[1]
    n_heads = a_log.shape[0]
    state_dim = (conv_w.shape[1] - d_inner) // 2
    nb = d_inner // LB
    npair = nb // 2
    n_chip = n_seq // 2
    hrows = state_dim // n_chip
    dims = (n_seq, n_tok, d_model, d_inner, n_heads, state_dim)
    dt_block = (2 * d_inner + 2 * state_dim) // LANES
    vmem = pl.BlockSpec(memory_space=pltpu.VMEM)
    anyspace = pl.BlockSpec(memory_space=pl.ANY)
    dma = pltpu.SemaphoreType.DMA
    scratch = [
        pltpu.VMEM((n_tok + HALO, d_model), BF16),
        pltpu.VMEM((3, d_model, LB), BF16),
        pltpu.VMEM((d_model, 2 * state_dim), BF16),
        pltpu.VMEM((nb, n_tok, LB), BF16),
        pltpu.VMEM((nb, n_tok, LB), BF16),
        pltpu.VMEM((nb, n_tok, LB), F32),
        pltpu.VMEM((n_tok + HALO, LB), F32),
        pltpu.VMEM((n_tok, LB), BF16),
        pltpu.VMEM((nb, state_dim, LB), F32),
        pltpu.VMEM((npair, state_dim, LB), F32),
        pltpu.VMEM((npair, 2, state_dim, LB), F32),
        pltpu.VMEM((npair, n_chip, hrows, LB), F32),
        pltpu.VMEM((npair, n_chip, hrows, LB), F32),
        pltpu.VMEM((npair, n_chip, hrows, LB), F32),
        pltpu.VMEM((npair, n_chip, hrows, LB), F32),
        pltpu.VMEM((npair, 2, state_dim, LB), F32),
        pltpu.VMEM((npair, state_dim, LB), F32),
        pltpu.VMEM((n_tok, 2 * state_dim), BF16),
        pltpu.VMEM((n_tok // CHUNK, state_dim, CHUNK), BF16),
        pltpu.VMEM((n_tok // CHUNK, CHUNK, CHUNK), F32),
        pltpu.VMEM((n_tok, LANES), F32),
        pltpu.VMEM((LANES, n_tok), F32),
        pltpu.VMEM((LANES, n_tok), F32),
        pltpu.VMEM((n_tok, LANES), F32),
        pltpu.VMEM((n_tok, LANES), F32),
        pltpu.VMEM((n_tok, LANES), F32),
        pltpu.VMEM((8, LANES), F32),
        pltpu.VMEM((8, LANES), F32),
        pltpu.VMEM((2, 8, LANES), F32),
        pltpu.VMEM((8, LANES), F32),
        pltpu.VMEM((n_chip, 8, LANES), F32),
        pltpu.VMEM((3, n_tok, LANES), F32),
        pltpu.VMEM((n_tok, LANES), F32),
        pltpu.VMEM((HALO, d_model), BF16),
        dma(()), dma((3,)), dma(()), dma(()), dma(()), dma(()), dma(()), dma(()), dma(()),
        dma((npair,)), dma((npair,)), dma((npair,)), dma((npair,)), dma((npair,)), dma((npair,)), dma((npair,)), dma((npair,)),
        dma((nb,)),
    ]
    return pl.pallas_call(
        functools.partial(mixer_kernel, dims),
        out_shape=jax.ShapeDtypeStruct((n_tok, d_inner), BF16),
        grid=(1,),
        in_specs=[anyspace, vmem, anyspace, pl.BlockSpec((d_model, LANES), lambda i: (0, dt_block), pipeline_mode=pl.Buffered(1)), vmem, vmem, vmem, vmem, vmem, vmem],
        out_specs=anyspace,
        scratch_shapes=scratch,
        compiler_params=pltpu.CompilerParams(collective_id=0, has_side_effects=True, vmem_limit_bytes=66 * 1000 * 1000),
        name='mixer',
    )(x, doc_start.reshape(n_tok // LANES, LANES), w_in, w_in, conv_w, conv_b.reshape(1, -1), dt_bias.reshape(1, -1),
      a_log.reshape(1, -1), d_skip.reshape(1, -1), norm_w.reshape(1, -1))


def solution(mesh):
    n_seq = mesh.shape['sp']
    row_spec = P(('dp', 'sp'), None)
    tok_spec = P(('dp', 'sp'))

    def layer_shard(x, doc_start, w_in, conv_w, conv_b, dt_bias, a_log, d_skip, norm_w, w_out):
        g = mixer(n_seq, x, doc_start, w_in, conv_w, conv_b, dt_bias, a_log, d_skip, norm_w)
        return jnp.dot(g, w_out, preferred_element_type=F32).astype(BF16)

    return jax.shard_map(layer_shard, mesh=mesh, in_specs=(row_spec, tok_spec, P(), P(), P(), P(), P(), P(), P(), P()), out_specs=row_spec, check_vma=False)
```

time: 524 us -> 188 us (0.36)
  waiting for transfers between devices: 226 us -> 0 us
  Pallas kernels: 0 us -> 99.8 us
  matrix products: 105 us -> 21.3 us
  starting transfers between devices: 59.1 us -> 0 us
  other arithmetic: 58.3 us -> 0 us
  local copies, waits for them, and re-layouts: 73 us -> 64.3 us
    ppermute x11 -> x0, waiting for transfers between devices: 226 us -> none  [the longest x4 142 us: layer_shard(): got_decay = lax.ppermute(acc_decay, 'sp', hop_pairs)]
    pallas_call x0 -> x1, Pallas kernels: none -> 99.8 us  [mixer(): pl.pallas_call(functools.partial(mixer_kernel, dims), out_shape=jax.Shape...]
    dot_general x7 -> x1, matrix products: 105 us -> 21.3 us  [layer_shard(): return jnp.dot(g, w_out, preferred_element_type=F32).astype(BF16)]
    ppermute x11 -> x0, starting transfers between devices: 59.1 us -> none  [the longest x5 25.8 us: layer_shard(): got_state = lax.ppermute(acc_state, 'sp', hop_pairs)]
    unnamed x37 -> x1, local copies, waits for them, and re-layouts: 4.91 us -> 63 us
    reshape x4 -> x1, local copies, waits for them, and re-layouts: 35.8 us -> 1.36 us  [mixer(): conv_b.reshape(1, -1)]
    convert_element_type x6 -> x0, other arithmetic: 23.3 us -> none  [the longest x1 17.1 us: causal_conv(): return jax.nn.silu(pre_act).astype(jnp.bfloat16)]
    slice x9 -> x0, local copies, waits for them, and re-layouts: 19.4 us -> none  [the longest x2 11.3 us: local_scan(): conv_out[:, :d_inner]]
  transfers between devices with their start and end apart: 11 -> 0, of which waited for: 7 -> 0; matrix products, arithmetic and copies ran while one was open for 7% -> 0% of each run, Pallas kernels for 0% -> 0%
where the time goes in v1:
time: 188 us; the launch traced here: 185 us
  Pallas kernels  99.8 us (53%)
  local copies, waits for them, and re-layouts  64.3 us (34%)
  matrix products  21.3 us (11%)
    pallas_call x1, Pallas kernels, mixer(): pl.pallas_call(functools.partial(mixer_kernel, dims), out_shape=jax.Shape...  99.8 us
    unnamed x1, local copies, waits for them, and re-layouts  63 us
    dot_general x1, matrix products, layer_shard(): return jnp.dot(g, w_out, preferred_element_type=F32).astype(BF16)  21.3 us

profile of v1, /device:TPU:97, one launch (start us, length us, event | category | flops | bytes accessed | tf_op | source)
XLA Modules:
  0.0 185.4 jit_solution(10838736403613511860)
XLA Ops:
  0.0 1.4 reshape.16.cb_ref
  1.4 63.0 %copy.11.w_hbm.wdt_ref = bf16[2560,10576]{1,0:T(8,128)(2,1)} copy(bf16[2560,10576]{0,1:T(8,128)(2,1)} %param.12) | data formatting | bytes 108298240 | tf_op args[2]
  64.3 99.8 %mixer.1 = bf16[512,5120]{1,0:T(8,128)(2,1)} custom-call(bf16[512,2560]{1,0:T(8,128)(2,1)} %x_hbm.1, s32[4,128]{1,0:T(4,128)} %bitcast.6, bf16[2560,10576]{1,0:T(8,128)(2,1)} %copy.11.w_hbm.wdt_ref, bf16[2560,10576]{1,0:T(8,128)(2,1)} %copy.11.w_hbm.wdt_ref, f32[4,5376]{1,0:T(4,128)} %cw_ref.1, f32[1,5376]{1,0:T(1,128)} %reshape.16.cb_ref, f32[1,80]{1,0:T(1,128)} %bitcast.7, ...), custom_call_target="tpu_custom_call" | custom-call | tf_op jit(solution)/shard_map/mixer/pallas_call | solution.py:525
  164.1 21.3 %convolution_convert_fusion = bf16[512,2560]{1,0:T(8,128)(2,1)} fusion(bf16[512,5120]{1,0:T(8,128)(2,1)} %mixer.1, bf16[5120,2560]{1,0:T(8,128)(2,1)} %param.19), kind=kOutput, calls=%fused_computation | convolution fusion | flops 13423083520 | bytes 34078720 | tf_op jit(solution)/shard_map/dot_general | solution.py:545

commit v2 on v1

--- a/solution.py
+++ b/solution.py
@@ -41,7 +41,7 @@
     return c + c * jnp.tanh(c)
 
 
-def mixer_kernel(dims, x_hbm, ds_ref, w_hbm, wdt_ref, cw_ref, cb_ref, dtb_ref, alog_ref, dsk_ref, nw_ref, g_hbm,
+def mixer_kernel(dims, x_hbm, ds_ref, w_hbm, cw_ref, cb_ref, dtb_ref, alog_ref, dsk_ref, nw_ref, g_hbm,
                  xe, wbuf, wbcd, zb, xb, yb, us, sc, cs0, tsend, two, tc, hrecv, hout, s0r, fbuf, soth,
                  bc, bt, gm, a2, apt, ldt, we, ws, arl, prm, dec, dpair, dchip, dg, mk, ssq, hal,
                  xsem, wsem, bsem, hs_sem, hr_sem, dp_sem, dps_sem, dg_sem, dgs_sem,
@@ -53,6 +53,7 @@
     npair = nb // 2
     n_chip = n_seq // 2
     hrows = state_dim // n_chip
+    n_bcd = 2 * state_dim + n_heads
     n_lt = LB // LANES
     n_zfirst = 2
 
@@ -75,7 +76,7 @@
 
     def wcopy(t):
         slot = lax.rem(t, 3)
-        return pltpu.make_async_copy(w_hbm.at[:, pl.ds(wcol(t), LB)], wbuf.at[slot], wsem.at[slot])
+        return pltpu.make_async_copy(w_hbm.at[pl.ds(wcol(t), LB)], wbuf.at[slot], wsem.at[slot])
 
     n_steps = 2 * nb
 
@@ -89,8 +90,9 @@
     xcopy = pltpu.make_async_copy(x_hbm, xe.at[pl.ds(HALO, n_tok)], xsem)
     xcopy.start()
     wcopy(jnp.int32(0)).start()
-    bcopy = pltpu.make_async_copy(w_hbm.at[:, pl.ds(2 * d_inner, 2 * state_dim)], wbcd, bsem)
+    bcopy = pltpu.make_async_copy(w_hbm.at[pl.ds(2 * d_inner, n_bcd)], wbcd.at[pl.ds(0, n_bcd)], bsem)
     bcopy.start()
+    wbcd[n_bcd:, :] = jnp.zeros((LANES - n_heads, d_model), BF16)
     wcopy(jnp.int32(1)).start()
 
     barrier = pltpu.get_barrier_semaphore()
@@ -135,7 +137,7 @@
         wnext(t)
         slot = lax.rem(t, 3)
         for q in range(n_tok // CHUNK):
-            zb[zi, q * CHUNK:(q + 1) * CHUNK] = dot(xe[HALO + q * CHUNK:HALO + (q + 1) * CHUNK], wbuf[slot]).astype(BF16)
+            zb[zi, q * CHUNK:(q + 1) * CHUNK] = dot_nt(xe[HALO + q * CHUNK:HALO + (q + 1) * CHUNK], wbuf[slot]).astype(BF16)
 
     pl.semaphore_wait(barrier, n_chip + 1)
     halo_send = pltpu.make_async_remote_copy(
@@ -159,11 +161,10 @@
         halo_send.wait_recv()
 
     bcopy.wait()
-    mrow = (n_tok + HALO) // 3
+    mrow = (n_tok + HALO) // 2
     lane = lax.broadcasted_iota(jnp.int32, (1, LANES), 1)
-    for q in range(3):
-        us[q * mrow:(q + 1) * mrow, 0:2 * state_dim] = dot(xe[q * mrow:(q + 1) * mrow], wbcd[...]).astype(BF16).astype(F32)
-        us[q * mrow:(q + 1) * mrow, 2 * state_dim:2 * state_dim + LANES] = dot(xe[q * mrow:(q + 1) * mrow], wdt_ref[...]).astype(BF16).astype(F32)
+    for q in range(2):
+        us[q * mrow:(q + 1) * mrow, 0:2 * state_dim + LANES] = dot_nt(xe[q * mrow:(q + 1) * mrow], wbcd[...]).astype(BF16).astype(F32)
 
     def conv(r0, lt, wl):
         cols = slice(lt * LANES, (lt + 1) * LANES)
@@ -260,8 +261,8 @@
     def ublock(t, b, t_ref):
         wnext(t)
         slot = lax.rem(t, 3)
-        for q in range(3):
-            us[q * mrow:(q + 1) * mrow, :] = dot(xe[q * mrow:(q + 1) * mrow], wbuf[slot]).astype(BF16).astype(F32)
+        for q in range(2):
+            us[q * mrow:(q + 1) * mrow, :] = dot_nt(xe[q * mrow:(q + 1) * mrow], wbuf[slot]).astype(BF16).astype(F32)
         roll_to(arl, we, b)
 
         @pl.loop(0, n_tok // ROWS)
@@ -479,14 +480,13 @@
     n_chip = n_seq // 2
     hrows = state_dim // n_chip
     dims = (n_seq, n_tok, d_model, d_inner, n_heads, state_dim)
-    dt_block = (2 * d_inner + 2 * state_dim) // LANES
     vmem = pl.BlockSpec(memory_space=pltpu.VMEM)
     anyspace = pl.BlockSpec(memory_space=pl.ANY)
     dma = pltpu.SemaphoreType.DMA
     scratch = [
         pltpu.VMEM((n_tok + HALO, d_model), BF16),
-        pltpu.VMEM((3, d_model, LB), BF16),
-        pltpu.VMEM((d_model, 2 * state_dim), BF16),
+        pltpu.VMEM((3, LB, d_model), BF16),
+        pltpu.VMEM((2 * state_dim + LANES, d_model), BF16),
         pltpu.VMEM((nb, n_tok, LB), BF16),
         pltpu.VMEM((nb, n_tok, LB), BF16),
         pltpu.VMEM((nb, n_tok, LB), F32),
@@ -525,13 +525,12 @@
     return pl.pallas_call(
         functools.partial(mixer_kernel, dims),
         out_shape=jax.ShapeDtypeStruct((n_tok, d_inner), BF16),
-        grid=(1,),
-        in_specs=[anyspace, vmem, anyspace, pl.BlockSpec((d_model, LANES), lambda i: (0, dt_block), pipeline_mode=pl.Buffered(1)), vmem, vmem, vmem, vmem, vmem, vmem],
+        in_specs=[anyspace, vmem, anyspace, vmem, vmem, vmem, vmem, vmem, vmem],
         out_specs=anyspace,
         scratch_shapes=scratch,
         compiler_params=pltpu.CompilerParams(collective_id=0, has_side_effects=True, vmem_limit_bytes=66 * 1000 * 1000),
         name='mixer',
-    )(x, doc_start.reshape(n_tok // LANES, LANES), w_in, w_in, conv_w, conv_b.reshape(1, -1), dt_bias.reshape(1, -1),
+    )(x, doc_start.reshape(n_tok // LANES, LANES), w_in.T, conv_w, conv_b.reshape(1, -1), dt_bias.reshape(1, -1),
       a_log.reshape(1, -1), d_skip.reshape(1, -1), norm_w.reshape(1, -1))
 
 

time: 188 us -> 124 us (0.66); the launches traced: 185 us -> 124 us
  local copies, waits for them, and re-layouts: 64.3 us -> 1.36 us
  Pallas kernels: 99.8 us -> 102 us
    unnamed x1 -> x0, local copies, waits for them, and re-layouts: 63 us -> none
where the time goes in v2:
time: 124 us
  Pallas kernels  102 us (82%)
  matrix products  21.4 us (17%)
  local copies, waits for them, and re-layouts  1.36 us (1%)
    pallas_call x1, Pallas kernels, mixer(): pl.pallas_call(functools.partial(mixer_kernel, dims), out_shape=jax.Shape...  102 us
    dot_general x1, matrix products, layer_shard(): return jnp.dot(g, w_out, preferred_element_type=F32).astype(BF16)  21.4 us

profile of v2, /device:TPU:97, one launch (start us, length us, event | category | flops | bytes accessed | tf_op | source)
XLA Modules:
  0.0 124.2 jit_solution(9443743292562213224)
XLA Ops:
  0.0 1.4 %reshape.16.cb_ref = f32[1,5376]{1,0:T(1,128)} reshape(f32[5376]{0:T(1024)} %param.14) | data formatting | bytes 43008 | tf_op jit(solution)/shard_map/reshape | solution.py:533
  1.4 101.5 %mixer.1 = bf16[512,5120]{1,0:T(8,128)(2,1)} custom-call(bf16[512,2560]{1,0:T(8,128)(2,1)} %x_hbm.1, s32[4,128]{1,0:T(4,128)} %bitcast.8, bf16[10576,2560]{1,0:T(8,128)(2,1)} %bitcast.7, f32[4,5376]{1,0:T(4,128)} %cw_ref.1, f32[1,5376]{1,0:T(1,128)} %reshape.16.cb_ref, f32[1,80]{1,0:T(1,128)} %bitcast.9, f32[1,80]{1,0:T(1,128)} %bitcast.10, ...), custom_call_target="tpu_custom_call" | custom-call | tf_op jit(solution)/shard_map/mixer/pallas_call | solution.py:525
  102.9 21.4 %convolution_convert_fusion = bf16[512,2560]{1,0:T(8,128)(2,1)} fusion(bf16[512,5120]{1,0:T(8,128)(2,1)} %mixer.1, bf16[5120,2560]{1,0:T(8,128)(2,1)} %param.19), kind=kOutput, calls=%fused_computation | convolution fusion | flops 13423083520 | bytes 34078720 | tf_op jit(solution)/shard_map/dot_general | solution.py:544

commit v3 on v2

--- a/solution.py
+++ b/solution.py
@@ -41,8 +41,8 @@
     return c + c * jnp.tanh(c)
 
 
-def mixer_kernel(dims, x_hbm, ds_ref, w_hbm, cw_ref, cb_ref, dtb_ref, alog_ref, dsk_ref, nw_ref, g_hbm,
-                 xe, wbuf, wbcd, zb, xb, yb, us, sc, cs0, tsend, two, tc, hrecv, hout, s0r, fbuf, soth,
+def mixer_kernel(dims, x_hbm, ds_ref, w_hbm, wo_hbm, cw_ref, cb_ref, dtb_ref, alog_ref, dsk_ref, nw_ref, o_hbm,
+                 xe, wbuf, wbcd, zb, xb, yb, us, us2, sc, mix, cs0, tsend, two, tc, hrecv, hout, s0r, fbuf, soth,
                  bc, bt, gm, a2, apt, ldt, we, ws, arl, prm, dec, dpair, dchip, dg, mk, ssq, hal,
                  xsem, wsem, bsem, hs_sem, hr_sem, dp_sem, dps_sem, dg_sem, dgs_sem,
                  ps_sem, pr_sem, s1_sem, r1_sem, s2_sem, r2_sem, fs_sem, fr_sem, gsem):
@@ -78,14 +78,20 @@
         slot = lax.rem(t, 3)
         return pltpu.make_async_copy(w_hbm.at[pl.ds(wcol(t), LB)], wbuf.at[slot], wsem.at[slot])
 
-    n_steps = 2 * nb
+    n_steps = 3 * nb
 
     def wnext(t):
-        wcopy(t).wait()
-
-        @pl.when(t + 2 < n_steps)
+        slot = lax.rem(t, 3)
+        pltpu.make_async_copy(w_hbm.at[pl.ds(0, LB)], wbuf.at[slot], wsem.at[slot]).wait()
+
+        @pl.when(t + 2 < 2 * nb)
         def _():
             wcopy(t + 2).start()
+
+        @pl.when(jnp.logical_and(t + 2 >= 2 * nb, t + 2 < n_steps))
+        def _():
+            slot = lax.rem(t + 2, 3)
+            pltpu.make_async_copy(wo_hbm.at[pl.ds(pl.multiple_of((t + 2 - 2 * nb) * LB, LB), LB)], wbuf.at[slot], wsem.at[slot]).start()
 
     xcopy = pltpu.make_async_copy(x_hbm, xe.at[pl.ds(HALO, n_tok)], xsem)
     xcopy.start()
@@ -164,23 +170,31 @@
     mrow = (n_tok + HALO) // 2
     lane = lax.broadcasted_iota(jnp.int32, (1, LANES), 1)
     for q in range(2):
-        us[q * mrow:(q + 1) * mrow, 0:2 * state_dim + LANES] = dot_nt(xe[q * mrow:(q + 1) * mrow], wbcd[...]).astype(BF16).astype(F32)
-
-    def conv(r0, lt, wl):
+        us2[q * mrow:(q + 1) * mrow, 0:2 * state_dim + LANES] = dot_nt(xe[q * mrow:(q + 1) * mrow], wbcd[...]).astype(BF16).astype(F32)
+
+    def udot(slot, u_ref, q):
+        u_ref[q * mrow:(q + 1) * mrow, :] = dot_nt(xe[q * mrow:(q + 1) * mrow], wbuf[slot]).astype(BF16).astype(F32)
+
+    t_u = n_zfirst
+    wnext(jnp.int32(t_u))
+    udot(t_u % 3, us, 0)
+    udot(t_u % 3, us, 1)
+
+    def conv(u_ref, r0, lt, wl):
         cols = slice(lt * LANES, (lt + 1) * LANES)
-        ext = us[pl.ds(pl.multiple_of(r0 + HALO - 8, 8), ROWS + 8), cols]
+        ext = u_ref[pl.ds(pl.multiple_of(r0 + HALO - 8, 8), ROWS + 8), cols]
         wl = pl.multiple_of(wl, LANES)
         cw = cw_ref[:, pl.ds(wl, LANES)] * 0.5
-        v = cb_ref[:, pl.ds(wl, LANES)] * 0.5 + cw[0:1] * ext[8:8 + ROWS]
+        v = cb_ref[pl.ds(wl // LANES, 1), :] * 0.5 + cw[0:1] * ext[8:8 + ROWS]
         for k in range(1, 4):
             v = v + cw[k:k + 1] * (mk[k - 1, pl.ds(r0, ROWS), :] * ext[8 - k:8 - k + ROWS])
         return half_silu(v)
 
-    @pl.loop(0, n_tok // ROWS)
+    @pl.loop(0, n_tok // ROWS, unroll=True)
     def _(q):
         r0 = pl.multiple_of(q * ROWS, ROWS)
         for lt in range(2 * state_dim // LANES):
-            bc[pl.ds(r0, ROWS), lt * LANES:(lt + 1) * LANES] = conv(r0, lt, d_inner + lt * LANES).astype(BF16)
+            bc[pl.ds(r0, ROWS), lt * LANES:(lt + 1) * LANES] = conv(us2, r0, lt, d_inner + lt * LANES).astype(BF16)
 
     prm[...] = jnp.zeros((8, LANES), F32)
     prm[0:1, 0:n_heads] = dtb_ref[...]
@@ -192,7 +206,7 @@
     e_rows = []
     for c in range(n_chunks):
         rows = slice(c * CHUNK, (c + 1) * CHUNK)
-        raw = jnp.where(head_ok, us[HALO + c * CHUNK:HALO + (c + 1) * CHUNK, 2 * state_dim:2 * state_dim + LANES], 0.0) + pv[0:1]
+        raw = jnp.where(head_ok, us2[HALO + c * CHUNK:HALO + (c + 1) * CHUNK, 2 * state_dim:2 * state_dim + LANES], 0.0) + pv[0:1]
         dt = jnp.maximum(raw, 0.0) + jnp.log1p(jnp.exp(-jnp.abs(raw)))
         s1, s2, s3 = split3(neg_a * dt * LOG2E)
         acum = dot(tri, s3) + dot(tri, s2) + dot(tri, s1)
@@ -223,18 +237,20 @@
         src_ref=dpair.at[core], dst_ref=dpair.at[core], send_sem=dps_sem, recv_sem=dp_sem,
         device_id=dev(partner), device_id_type=MESH)
     pair_send.start()
-    pair_send.wait()
-    dchip[...] = dpair[0] * dpair[1]
-    dg[chip] = dpair[0] * dpair[1]
-    dec[2:3, :] = dpair[0][0:1]
-    dec[3:4, :] = dpair[1][0:1]
-
-    @pl.loop(1, n_chip)
-    def _(r):
-        q = lax.rem(chip + r, n_chip)
-        pltpu.make_async_remote_copy(
-            src_ref=dchip, dst_ref=dg.at[chip], send_sem=dgs_sem, recv_sem=dg_sem,
-            device_id=dev(2 * q + core), device_id_type=MESH).start()
+
+    def send_decays():
+        pair_send.wait()
+        dchip[...] = dpair[0] * dpair[1]
+        dg[chip] = dpair[0] * dpair[1]
+        dec[2:3, :] = dpair[0][0:1]
+        dec[3:4, :] = dpair[1][0:1]
+
+        @pl.loop(1, n_chip)
+        def _(r):
+            q = lax.rem(chip + r, n_chip)
+            pltpu.make_async_remote_copy(
+                src_ref=dchip, dst_ref=dg.at[chip], send_sem=dgs_sem, recv_sem=dg_sem,
+                device_id=dev(2 * q + core), device_id_type=MESH).start()
 
     def expand(v, b):
         n = v.shape[0]
@@ -258,21 +274,21 @@
         return jnp.where(low_r, jnp.broadcast_to(wv[:, 2 * lt:2 * lt + 1], (ROWS, LANES)),
                          jnp.broadcast_to(wv[:, 2 * lt + 1:2 * lt + 2], (ROWS, LANES)))
 
-    def ublock(t, b, t_ref):
-        wnext(t)
-        slot = lax.rem(t, 3)
-        for q in range(2):
-            us[q * mrow:(q + 1) * mrow, :] = dot_nt(xe[q * mrow:(q + 1) * mrow], wbuf[slot]).astype(BF16).astype(F32)
+    def ublock(t_next, u_next, u_ref, b, t_ref):
+        wnext(t_next)
+        slot = lax.rem(t_next, 3)
         roll_to(arl, we, b)
-
-        @pl.loop(0, n_tok // ROWS)
-        def _(q):
-            r0 = pl.multiple_of(q * ROWS, ROWS)
-            for lt in range(n_lt):
-                cols = slice(lt * LANES, (lt + 1) * LANES)
-                xs = conv(r0, lt, b * LB + lt * LANES).astype(BF16)
-                xb[b, pl.ds(r0, ROWS), cols] = xs
-                sc[pl.ds(r0, ROWS), cols] = (xs.astype(F32) * head_cols(r0, lt)).astype(BF16)
+        for half in range(2):
+            udot(slot, u_next, half)
+
+            @pl.loop(0, n_tok // ROWS // 2, unroll=True)
+            def _(q):
+                r0 = pl.multiple_of(half * (n_tok // 2) + q * ROWS, ROWS)
+                for lt in range(n_lt):
+                    cols = slice(lt * LANES, (lt + 1) * LANES)
+                    xs = conv(u_ref, r0, lt, b * LB + lt * LANES).astype(BF16)
+                    xb[b, pl.ds(r0, ROWS), cols] = xs
+                    sc[pl.ds(r0, ROWS), cols] = (xs.astype(F32) * head_cols(r0, lt)).astype(BF16)
 
         ex = expand(dec[...], b)
         st0 = dot(bt[0], sc[0:CHUNK])
@@ -342,9 +358,14 @@
     @pl.loop(0, npair)
     def _(i):
         t = n_zfirst + 2 * i
-        ublock(t, 2 * i + 1 - core, tsend.at[i])
+        ublock(t + 1, us2, us, 2 * i + 1 - core, tsend.at[i])
         part_copy(i).start()
-        ublock(t + 1, 2 * i + core, two.at[i, core])
+
+        @pl.when(i == 0)
+        def _():
+            send_decays()
+
+        ublock(t + 2, us, us2, 2 * i + core, two.at[i, core])
         send_home(i, 2 * i + core)
 
         @pl.when(i == 0)
@@ -358,53 +379,70 @@
         @pl.when(i >= 2)
         def _():
             finish(i - 2)
+
+    zb[n_zfirst] = us[HALO:HALO + n_tok, :].astype(BF16)
 
     low_b = (lax.broadcasted_iota(jnp.int32, (CHUNK, LANES), 1) < head_dim).astype(F32).astype(BF16)
     high_b = (lax.broadcasted_iota(jnp.int32, (CHUNK, LANES), 1) >= head_dim).astype(F32).astype(BF16)
 
+    sub = 32
+
     def intra(b):
-        roll_to(arl, a2, b)
-        hrows8 = pl.ds(pl.multiple_of(b * hb, hb), hb)
+        heads = pl.ds(pl.multiple_of(b * hb, hb), hb)
         dsk = expand(prm[...], b)[2:3]
         for c in range(n_chunks):
             r0 = c * CHUNK
+            ap8 = apt[heads, r0:r0 + CHUNK]
+            ld8 = ldt[heads, r0:r0 + CHUNK]
             for p in range(n_lt):
                 cols = slice(p * LANES, (p + 1) * LANES)
-                lhs0, lhs1 = [], []
-                for h in (2 * p, 2 * p + 1):
-                    ai0 = jnp.broadcast_to(arl[r0:r0 + HALF, h:h + 1], (HALF, HALF))
-                    ai1 = jnp.broadcast_to(arl[r0 + HALF:r0 + CHUNK, h:h + 1], (HALF, HALF))
-                    aj = apt[hrows8, r0:r0 + CHUNK][h:h + 1]
-                    ld = ldt[hrows8, r0:r0 + CHUNK][h:h + 1]
-                    lhs0.append((jnp.exp2(jnp.minimum(ai0 - aj[:, :HALF], ld[:, :HALF])) * gm[c, 0:HALF, 0:HALF]).astype(BF16))
-                    lhs1.append((jnp.exp2(ai1 - aj[:, :HALF]) * gm[c, HALF:CHUNK, 0:HALF]).astype(BF16))
-                    lhs1.append((jnp.exp2(jnp.minimum(ai1 - aj[:, HALF:], ld[:, HALF:])) * gm[c, HALF:CHUNK, HALF:CHUNK]).astype(BF16))
+                k = p % 4
+                for hh in range(2):
+                    h = 2 * p + hh
+                    aj0, aj1 = ap8[h:h + 1, :HALF], ap8[h:h + 1, HALF:]
+                    ld0, ld1 = ld8[h:h + 1, :HALF], ld8[h:h + 1, HALF:]
+                    base = CHUNK + hh * CHUNK
+                    for q in range(HALF // sub):
+                        rr = slice(q * sub, (q + 1) * sub)
+                        g0 = slice(q * sub, (q + 1) * sub)
+                        g1 = slice(HALF + q * sub, HALF + (q + 1) * sub)
+                        ai0 = jnp.broadcast_to(arl[r0 + q * sub:r0 + (q + 1) * sub, h:h + 1], (sub, HALF))
+                        ai1 = jnp.broadcast_to(arl[r0 + HALF + q * sub:r0 + HALF + (q + 1) * sub, h:h + 1], (sub, HALF))
+                        mix[k, rr, hh * HALF:(hh + 1) * HALF] = (jnp.exp2(jnp.minimum(ai0 - aj0, ld0)) * gm[c, g0, 0:HALF]).astype(BF16)
+                        mix[k, rr, base:base + HALF] = (jnp.exp2(ai1 - aj0) * gm[c, g1, 0:HALF]).astype(BF16)
+                        mix[k, rr, base + HALF:base + CHUNK] = (jnp.exp2(jnp.minimum(ai1 - aj1, ld1)) * gm[c, g1, HALF:CHUNK]).astype(BF16)
                 xp = xb[b, r0:r0 + CHUNK, cols]
                 xa, xh = xp * low_b, xp * high_b
-                y0 = dot(jnp.concatenate(lhs0, axis=1), jnp.concatenate([xa[:HALF], xh[:HALF]], axis=0))
-                y1 = dot(jnp.concatenate(lhs1, axis=1), jnp.concatenate([xa, xh], axis=0))
+                y0 = dot(mix[k, :, 0:CHUNK], jnp.concatenate([xa[:HALF], xh[:HALF]], axis=0))
+                y1 = dot(mix[k, :, CHUNK:3 * CHUNK], jnp.concatenate([xa, xh], axis=0))
                 yb[b, r0:r0 + HALF, cols] = y0 + dsk[:, cols] * xp[:HALF].astype(F32)
                 yb[b, r0 + HALF:r0 + CHUNK, cols] = y1 + dsk[:, cols] * xp[HALF:].astype(F32)
 
-    @pl.loop(0, nb)
+    n_with = nb - n_zfirst - 1
+
+    @pl.loop(0, n_with)
     def _(m):
+        t = m + n_zfirst + 1 + nb
+        wnext(t)
+        slot = lax.rem(t, 3)
+        roll_to(arl, a2, m)
+        for q in range(n_tok // CHUNK):
+            zb[m + n_zfirst + 1, q * CHUNK:(q + 1) * CHUNK] = dot_nt(xe[HALO + q * CHUNK:HALO + (q + 1) * CHUNK], wbuf[slot]).astype(BF16)
         intra(m)
 
-        @pl.when(m < nb - n_zfirst)
-        def _():
-            zblock(m + n_zfirst + nb, m + n_zfirst)
-
-        @pl.when(m == 0)
+        @pl.when(m == 1)
         def _():
             home(npair - 1)
-
-        @pl.when(m == 1)
-        def _():
             finish(npair - 2)
 
-        @pl.when(m == nb - 5)
+        @pl.when(m == n_with - 1)
         def _():
             finish(npair - 1)
+
+    @pl.loop(n_with, nb)
+    def _(m):
+        roll_to(arl, a2, m)
+        intra(m)
 
     ssq[...] = jnp.zeros((n_tok, LANES), F32)
 
@@ -416,7 +454,7 @@
         s_mid = ex[0:1] * s_in + cs0[b]
         us[CHUNK:2 * CHUNK, :] = dot(bc[CHUNK:2 * CHUNK, state_dim:2 * state_dim], s_mid.astype(BF16))
 
-        @pl.loop(0, n_tok // ROWS)
+        @pl.loop(0, n_tok // ROWS, unroll=True)
         def _(q):
             rows = pl.ds(pl.multiple_of(q * ROWS, ROWS), ROWS)
             acc = ssq[rows, :]
@@ -437,12 +475,10 @@
     scale = lax.rsqrt(jnp.sum(ssq[...], axis=1, keepdims=True) * (1.0 / d_inner) + EPS)
     ssq[...] = jnp.broadcast_to(scale, (n_tok, LANES))
 
-    def gcopy(b):
-        return pltpu.make_async_copy(zb.at[b], g_hbm.at[:, pl.ds(pl.multiple_of(b * LB, LB), LB)], gsem.at[b])
-
-    @pl.loop(0, nb)
-    def _(b):
-        @pl.loop(0, n_tok // ROWS)
+    n_out = d_model // LB
+
+    def normalize(b):
+        @pl.loop(0, n_tok // ROWS, unroll=True)
         def _(q):
             rows = pl.ds(pl.multiple_of(q * ROWS, ROWS), ROWS)
             sv = ssq[rows, :]
@@ -450,7 +486,38 @@
                 cols = slice(lt * LANES, (lt + 1) * LANES)
                 nw = nw_ref[:, pl.ds(pl.multiple_of(b * LB + lt * LANES, LANES), LANES)]
                 zb[b, rows, cols] = (yb[b, rows, cols] * sv * nw).astype(BF16)
-        gcopy(b).start()
+
+    @pl.loop(0, n_out)
+    def _(b):
+        normalize(b)
+
+    def project(b, first, last):
+        wnext(b + 2 * nb)
+        slot = lax.rem(b + 2 * nb, 3)
+        for n in range(n_out):
+            part = dot(zb[b], wbuf[slot, :, n * LB:(n + 1) * LB])
+            if not first:
+                part = yb[n] + part
+            if last:
+                xb[n] = part.astype(BF16)
+            else:
+                yb[n] = part
+
+    def ocopy(n):
+        return pltpu.make_async_copy(xb.at[n], o_hbm.at[:, n * LB:(n + 1) * LB], gsem.at[n])
+
+    project(jnp.int32(0), True, False)
+
+    @pl.loop(1, nb - 1)
+    def _(b):
+        @pl.when(b >= n_out - 1)
+        def _():
+            normalize(b + 1)
+        project(b, False, False)
+
+    project(jnp.int32(nb - 1), False, True)
+    for n in range(n_out):
+        ocopy(n).start()
 
     @pl.when(me < n_seq - 1)
     def _():
@@ -465,12 +532,11 @@
         all_copies(hout.at[i], s0r.at[i], s2_sem.at[i], r2_sem.at[i]).wait_send()
         fin_copy(i).wait_send()
 
-    @pl.loop(0, nb)
-    def _(b):
-        gcopy(b).wait()
-
-
-def mixer(n_seq, x, doc_start, w_in, conv_w, conv_b, dt_bias, a_log, d_skip, norm_w):
+    for n in range(n_out):
+        ocopy(n).wait()
+
+
+def mixer(n_seq, x, doc_start, w_in, conv_w, conv_b, dt_bias, a_log, d_skip, norm_w, w_out):
     n_tok, d_model = x.shape
     d_inner = norm_w.shape[0] * norm_w.shape[1]
     n_heads = a_log.shape[0]
@@ -491,7 +557,9 @@
         pltpu.VMEM((nb, n_tok, LB), BF16),
         pltpu.VMEM((nb, n_tok, LB), F32),
         pltpu.VMEM((n_tok + HALO, LB), F32),
+        pltpu.VMEM((n_tok + HALO, LB), F32),
         pltpu.VMEM((n_tok, LB), BF16),
+        pltpu.VMEM((4, HALF, 3 * CHUNK), BF16),
         pltpu.VMEM((nb, state_dim, LB), F32),
         pltpu.VMEM((npair, state_dim, LB), F32),
         pltpu.VMEM((npair, 2, state_dim, LB), F32),
@@ -520,17 +588,17 @@
         pltpu.VMEM((HALO, d_model), BF16),
         dma(()), dma((3,)), dma(()), dma(()), dma(()), dma(()), dma(()), dma(()), dma(()),
         dma((npair,)), dma((npair,)), dma((npair,)), dma((npair,)), dma((npair,)), dma((npair,)), dma((npair,)), dma((npair,)),
-        dma((nb,)),
+        dma((d_model // LB,)),
     ]
     return pl.pallas_call(
         functools.partial(mixer_kernel, dims),
-        out_shape=jax.ShapeDtypeStruct((n_tok, d_inner), BF16),
-        in_specs=[anyspace, vmem, anyspace, vmem, vmem, vmem, vmem, vmem, vmem],
+        out_shape=jax.ShapeDtypeStruct((n_tok, d_model), BF16),
+        in_specs=[anyspace, vmem, anyspace, anyspace, vmem, vmem, vmem, vmem, vmem, vmem],
         out_specs=anyspace,
         scratch_shapes=scratch,
         compiler_params=pltpu.CompilerParams(collective_id=0, has_side_effects=True, vmem_limit_bytes=66 * 1000 * 1000),
         name='mixer',
-    )(x, doc_start.reshape(n_tok // LANES, LANES), w_in.T, conv_w, conv_b.reshape(1, -1), dt_bias.reshape(1, -1),
+    )(x, doc_start.reshape(n_tok // LANES, LANES), w_in.T, w_out, conv_w, conv_b.reshape(-1, LANES), dt_bias.reshape(1, -1),
       a_log.reshape(1, -1), d_skip.reshape(1, -1), norm_w.reshape(1, -1))
 
 
@@ -540,7 +608,6 @@
     tok_spec = P(('dp', 'sp'))
 
     def layer_shard(x, doc_start, w_in, conv_w, conv_b, dt_bias, a_log, d_skip, norm_w, w_out):
-        g = mixer(n_seq, x, doc_start, w_in, conv_w, conv_b, dt_bias, a_log, d_skip, norm_w)
-        return jnp.dot(g, w_out, preferred_element_type=F32).astype(BF16)
+        return mixer(n_seq, x, doc_start, w_in, conv_w, conv_b, dt_bias, a_log, d_skip, norm_w, w_out)
 
     return jax.shard_map(layer_shard, mesh=mesh, in_specs=(row_spec, tok_spec, P(), P(), P(), P(), P(), P(), P(), P()), out_specs=row_spec, check_vma=False)

time: 124 us -> 103 us (0.83); the launches traced: 124 us -> 102 us
  matrix products: 21.4 us -> 0 us
  Pallas kernels: 102 us -> 98.2 us
  local copies, waits for them, and re-layouts: 1.36 us -> 3.4 us
    dot_general x1 -> x0, matrix products: 21.4 us -> none  [layer_shard(): return jnp.dot(g, w_out, preferred_element_type=F32).astype(BF16)]
    unnamed x0 -> x1, local copies, waits for them, and re-layouts: none -> 3.4 us
    pallas_call x1, Pallas kernels: 102 us -> 98.2 us  [mixer(): pl.pallas_call(functools.partial(mixer_kernel, dims), out_shape=jax.Shape...]
    reshape x1 -> x0, local copies, waits for them, and re-layouts: 1.36 us -> none  [mixer(): conv_b.reshape(1, -1)]
where the time goes in v3:
time: 103 us; the launch traced here: 102 us
  Pallas kernels  98.2 us (95%)
  local copies, waits for them, and re-layouts  3.4 us (3%)
    pallas_call x1, Pallas kernels, mixer(): pl.pallas_call(functools.partial(mixer_kernel, dims), out_shape=jax.Shape...  98.2 us
    unnamed x1, local copies, waits for them, and re-layouts  3.4 us

profile of v3, /device:TPU:97, one launch (start us, length us, event | category | flops | bytes accessed | tf_op | source)
XLA Modules:
  0.0 101.6 jit_solution(7664395651849108274)
XLA Ops:
  0.0 98.2 %mixer.1 = bf16[512,2560]{1,0:T(8,128)(2,1)} custom-call(bf16[512,2560]{1,0:T(8,128)(2,1)} %x_hbm.1, s32[4,128]{1,0:T(4,128)} %bitcast.8, bf16[10576,2560]{1,0:T(8,128)(2,1)} %bitcast.6, bf16[5120,2560]{1,0:T(8,128)(2,1)} %wo_hbm.1, f32[4,5376]{1,0:T(4,128)} %cw_ref.1, f32[42,128]{1,0:T(8,128)} %bitcast.7, f32[1,80]{1,0:T(1,128)} %bitcast.9, ...), custom_call_target="tpu_custom_call" | custom-call | tf_op jit(solution)/shard_map/mixer/pallas_call | solution.py:593
  98.2 3.4 %copy.12 = bf16[512,2560]{1,0:T(8,128)(2,1)} copy(bf16[512,2560]{1,0:T(8,128)(2,1)} %mixer.1) | data formatting | bytes 5242880

commit v4 on v3

--- a/solution.py
+++ b/solution.py
@@ -42,7 +42,7 @@
 
 
 def mixer_kernel(dims, x_hbm, ds_ref, w_hbm, wo_hbm, cw_ref, cb_ref, dtb_ref, alog_ref, dsk_ref, nw_ref, o_hbm,
-                 xe, wbuf, wbcd, zb, xb, yb, us, us2, sc, mix, cs0, tsend, two, tc, hrecv, hout, s0r, fbuf, soth,
+                 xe, wbuf, wbcd, zb, xb, yb, us, us2, yst, sc, mix, cs0, tsend, two, tc, hrecv, hout, s0r, fbuf, soth,
                  bc, bt, gm, a2, apt, ldt, we, ws, arl, prm, dec, dpair, dchip, dg, mk, ssq, hal,
                  xsem, wsem, bsem, hs_sem, hr_sem, dp_sem, dps_sem, dg_sem, dgs_sem,
                  ps_sem, pr_sem, s1_sem, r1_sem, s2_sem, r2_sem, fs_sem, fr_sem, gsem):
@@ -56,6 +56,9 @@
     n_bcd = 2 * state_dim + n_heads
     n_lt = LB // LANES
     n_zfirst = 2
+    t_z = n_zfirst + nb
+    n_zmid = npair - 2
+    n_zlast = npair - 1
 
     me = lax.axis_index('sp')
     chip = me // 2
@@ -70,8 +73,9 @@
         pair = i2 // 2
         own = lax.rem(i2, 2)
         ub = 2 * pair + jnp.where(own == 0, 1 - core, core)
+        zi = jnp.where(t <= t_z, n_zfirst, jnp.where(t <= t_z + n_zmid, n_zfirst + 2 * (t - t_z), n_zfirst + 1 + 2 * (t - t_z - n_zmid - 1)))
         col = jnp.where(t < n_zfirst, t * LB,
-                        jnp.where(t < n_zfirst + nb, d_inner + ub * LB, (t - nb) * LB))
+                        jnp.where(t < n_zfirst + nb, d_inner + ub * LB, zi * LB))
         return pl.multiple_of(col, LB)
 
     def wcopy(t):
@@ -142,8 +146,7 @@
     def zblock(t, zi):
         wnext(t)
         slot = lax.rem(t, 3)
-        for q in range(n_tok // CHUNK):
-            zb[zi, q * CHUNK:(q + 1) * CHUNK] = dot_nt(xe[HALO + q * CHUNK:HALO + (q + 1) * CHUNK], wbuf[slot]).astype(BF16)
+        zb[zi] = dot_nt(xe[HALO:HALO + n_tok], wbuf[slot]).astype(BF16)
 
     pl.semaphore_wait(barrier, n_chip + 1)
     halo_send = pltpu.make_async_remote_copy(
@@ -167,34 +170,31 @@
         halo_send.wait_recv()
 
     bcopy.wait()
-    mrow = (n_tok + HALO) // 2
     lane = lax.broadcasted_iota(jnp.int32, (1, LANES), 1)
-    for q in range(2):
-        us2[q * mrow:(q + 1) * mrow, 0:2 * state_dim + LANES] = dot_nt(xe[q * mrow:(q + 1) * mrow], wbcd[...]).astype(BF16).astype(F32)
-
-    def udot(slot, u_ref, q):
-        u_ref[q * mrow:(q + 1) * mrow, :] = dot_nt(xe[q * mrow:(q + 1) * mrow], wbuf[slot]).astype(BF16).astype(F32)
+    p_bcd = dot_nt(xe[...], wbcd[...]).astype(BF16).astype(F32)
+    for lt in range(2 * state_dim // LANES + 1):
+        us2[lt] = p_bcd[:, lt * LANES:(lt + 1) * LANES]
+
+    def udot(slot, u_ref):
+        p_u = dot_nt(xe[...], wbuf[slot]).astype(BF16).astype(F32)
+        for lt in range(n_lt):
+            u_ref[lt] = p_u[:, lt * LANES:(lt + 1) * LANES]
 
     t_u = n_zfirst
     wnext(jnp.int32(t_u))
-    udot(t_u % 3, us, 0)
-    udot(t_u % 3, us, 1)
+    udot(t_u % 3, us)
 
     def conv(u_ref, r0, lt, wl):
-        cols = slice(lt * LANES, (lt + 1) * LANES)
-        ext = u_ref[pl.ds(pl.multiple_of(r0 + HALO - 8, 8), ROWS + 8), cols]
         wl = pl.multiple_of(wl, LANES)
         cw = cw_ref[:, pl.ds(wl, LANES)] * 0.5
-        v = cb_ref[pl.ds(wl // LANES, 1), :] * 0.5 + cw[0:1] * ext[8:8 + ROWS]
+        v = cb_ref[pl.ds(wl // LANES, 1), :] * 0.5 + cw[0:1] * u_ref[lt, pl.ds(r0 + HALO, ROWS), :]
         for k in range(1, 4):
-            v = v + cw[k:k + 1] * (mk[k - 1, pl.ds(r0, ROWS), :] * ext[8 - k:8 - k + ROWS])
+            v = v + cw[k:k + 1] * (mk[k - 1, pl.ds(r0, ROWS), :] * u_ref[lt, pl.ds(r0 + HALO - k, ROWS), :])
         return half_silu(v)
 
-    @pl.loop(0, n_tok // ROWS, unroll=True)
-    def _(q):
-        r0 = pl.multiple_of(q * ROWS, ROWS)
+    for r0 in range(0, n_tok, ROWS):
         for lt in range(2 * state_dim // LANES):
-            bc[pl.ds(r0, ROWS), lt * LANES:(lt + 1) * LANES] = conv(us2, r0, lt, d_inner + lt * LANES).astype(BF16)
+            bc[r0:r0 + ROWS, lt * LANES:(lt + 1) * LANES] = conv(us2, r0, lt, d_inner + lt * LANES).astype(BF16)
 
     prm[...] = jnp.zeros((8, LANES), F32)
     prm[0:1, 0:n_heads] = dtb_ref[...]
@@ -206,7 +206,7 @@
     e_rows = []
     for c in range(n_chunks):
         rows = slice(c * CHUNK, (c + 1) * CHUNK)
-        raw = jnp.where(head_ok, us2[HALO + c * CHUNK:HALO + (c + 1) * CHUNK, 2 * state_dim:2 * state_dim + LANES], 0.0) + pv[0:1]
+        raw = jnp.where(head_ok, us2[2 * state_dim // LANES, HALO + c * CHUNK:HALO + (c + 1) * CHUNK, :], 0.0) + pv[0:1]
         dt = jnp.maximum(raw, 0.0) + jnp.log1p(jnp.exp(-jnp.abs(raw)))
         s1, s2, s3 = split3(neg_a * dt * LOG2E)
         acum = dot(tri, s3) + dot(tri, s2) + dot(tri, s1)
@@ -278,17 +278,13 @@
         wnext(t_next)
         slot = lax.rem(t_next, 3)
         roll_to(arl, we, b)
-        for half in range(2):
-            udot(slot, u_next, half)
-
-            @pl.loop(0, n_tok // ROWS // 2, unroll=True)
-            def _(q):
-                r0 = pl.multiple_of(half * (n_tok // 2) + q * ROWS, ROWS)
-                for lt in range(n_lt):
-                    cols = slice(lt * LANES, (lt + 1) * LANES)
-                    xs = conv(u_ref, r0, lt, b * LB + lt * LANES).astype(BF16)
-                    xb[b, pl.ds(r0, ROWS), cols] = xs
-                    sc[pl.ds(r0, ROWS), cols] = (xs.astype(F32) * head_cols(r0, lt)).astype(BF16)
+        udot(slot, u_next)
+        for r0 in range(0, n_tok, ROWS):
+            for lt in range(n_lt):
+                cols = slice(lt * LANES, (lt + 1) * LANES)
+                xs = conv(u_ref, r0, lt, b * LB + lt * LANES).astype(BF16)
+                xb[b, r0:r0 + ROWS, cols] = xs
+                sc[r0:r0 + ROWS, cols] = (xs.astype(F32) * head_cols(r0, lt)).astype(BF16)
 
         ex = expand(dec[...], b)
         st0 = dot(bt[0], sc[0:CHUNK])
@@ -328,7 +324,7 @@
             tc[i, q] = ex[3:4] * two[i, 0, rows] + two[i, 1, rows]
         hrecv[i, chip] = tc[i, chip]
 
-        @pl.loop(1, n_chip)
+        @pl.loop(1, n_chip, unroll=True)
         def _(r):
             home_copy(i, lax.rem(chip + r, n_chip)).start()
 
@@ -341,7 +337,7 @@
             run = expand(dg[q], b)[0:1] * run + hrecv[i, q]
         s0r[i, chip] = hout[i, chip]
 
-        @pl.loop(1, n_chip)
+        @pl.loop(1, n_chip, unroll=True)
         def _(r):
             back_copy(i, lax.rem(chip + r, n_chip)).start()
 
@@ -376,11 +372,12 @@
         def _():
             home(i - 1)
 
-        @pl.when(i >= 2)
-        def _():
-            finish(i - 2)
-
-    zb[n_zfirst] = us[HALO:HALO + n_tok, :].astype(BF16)
+        @pl.when(i >= 3)
+        def _():
+            finish(i - 3)
+
+    for lt in range(n_lt):
+        zb[n_zfirst, :, lt * LANES:(lt + 1) * LANES] = us[lt, HALO:HALO + n_tok, :].astype(BF16)
 
     low_b = (lax.broadcasted_iota(jnp.int32, (CHUNK, LANES), 1) < head_dim).astype(F32).astype(BF16)
     high_b = (lax.broadcasted_iota(jnp.int32, (CHUNK, LANES), 1) >= head_dim).astype(F32).astype(BF16)
@@ -418,31 +415,34 @@
                 yb[b, r0:r0 + HALF, cols] = y0 + dsk[:, cols] * xp[:HALF].astype(F32)
                 yb[b, r0 + HALF:r0 + CHUNK, cols] = y1 + dsk[:, cols] * xp[HALF:].astype(F32)
 
-    n_with = nb - n_zfirst - 1
-
-    @pl.loop(0, n_with)
+    def zdot(t, zi):
+        slot = lax.rem(t, 3)
+        zb[zi] = dot_nt(xe[HALO:HALO + n_tok], wbuf[slot]).astype(BF16)
+
+    @pl.loop(0, n_zmid)
     def _(m):
-        t = m + n_zfirst + 1 + nb
+        t = t_z + 1 + m
         wnext(t)
-        slot = lax.rem(t, 3)
         roll_to(arl, a2, m)
-        for q in range(n_tok // CHUNK):
-            zb[m + n_zfirst + 1, q * CHUNK:(q + 1) * CHUNK] = dot_nt(xe[HALO + q * CHUNK:HALO + (q + 1) * CHUNK], wbuf[slot]).astype(BF16)
+        zdot(t, n_zfirst + 2 * (m + 1))
         intra(m)
 
-        @pl.when(m == 1)
+        @pl.when(m == 0)
+        def _():
+            finish(npair - 3)
+
+        @pl.when(m == n_zmid - 1)
         def _():
             home(npair - 1)
-            finish(npair - 2)
-
-        @pl.when(m == n_with - 1)
-        def _():
-            finish(npair - 1)
-
-    @pl.loop(n_with, nb)
+
+    @pl.loop(n_zmid, nb)
     def _(m):
         roll_to(arl, a2, m)
         intra(m)
+
+        @pl.when(m == nb - 4)
+        def _():
+            finish(npair - 2)
 
     ssq[...] = jnp.zeros((n_tok, LANES), F32)
 
@@ -450,9 +450,9 @@
         ex = expand(dec[...], b)
         roll_to(arl, ws, b)
         s_in = s_ref[...]
-        us[0:CHUNK, :] = dot(bc[0:CHUNK, state_dim:2 * state_dim], s_in.astype(BF16))
+        yst[0:CHUNK, :] = dot(bc[0:CHUNK, state_dim:2 * state_dim], s_in.astype(BF16))
         s_mid = ex[0:1] * s_in + cs0[b]
-        us[CHUNK:2 * CHUNK, :] = dot(bc[CHUNK:2 * CHUNK, state_dim:2 * state_dim], s_mid.astype(BF16))
+        yst[CHUNK:2 * CHUNK, :] = dot(bc[CHUNK:2 * CHUNK, state_dim:2 * state_dim], s_mid.astype(BF16))
 
         @pl.loop(0, n_tok // ROWS, unroll=True)
         def _(q):
@@ -460,7 +460,7 @@
             acc = ssq[rows, :]
             for lt in range(n_lt):
                 cols = slice(lt * LANES, (lt + 1) * LANES)
-                y = yb[b, rows, cols] + head_cols(q * ROWS, lt) * us[rows, cols]
+                y = yb[b, rows, cols] + head_cols(q * ROWS, lt) * yst[rows, cols]
                 gated = y * half_silu(zb[b, rows, cols].astype(F32) * 0.5)
                 yb[b, rows, cols] = gated
                 acc = acc + gated * gated
@@ -468,9 +468,20 @@
 
     @pl.loop(0, npair)
     def _(i):
+        fin_copy(i).wait_recv()
+        t = t_z + n_zmid + 1 + i
+
+        @pl.when(i < n_zlast)
+        def _():
+            wnext(t)
+
+        zdot(jnp.minimum(t, 2 * nb - 1), jnp.where(i < n_zlast, n_zfirst + 1 + 2 * i, nb))
         close(2 * i + core, fbuf.at[i, core])
-        fin_copy(i).wait_recv()
         close(2 * i + 1 - core, soth.at[i])
+
+        @pl.when(i == npair - 3)
+        def _():
+            finish(npair - 1)
 
     scale = lax.rsqrt(jnp.sum(ssq[...], axis=1, keepdims=True) * (1.0 / d_inner) + EPS)
     ssq[...] = jnp.broadcast_to(scale, (n_tok, LANES))
@@ -553,11 +564,12 @@
         pltpu.VMEM((n_tok + HALO, d_model), BF16),
         pltpu.VMEM((3, LB, d_model), BF16),
         pltpu.VMEM((2 * state_dim + LANES, d_model), BF16),
-        pltpu.VMEM((nb, n_tok, LB), BF16),
+        pltpu.VMEM((nb + 1, n_tok, LB), BF16),
         pltpu.VMEM((nb, n_tok, LB), BF16),
         pltpu.VMEM((nb, n_tok, LB), F32),
-        pltpu.VMEM((n_tok + HALO, LB), F32),
-        pltpu.VMEM((n_tok + HALO, LB), F32),
+        pltpu.VMEM((LB // LANES, n_tok + HALO, LANES), F32),
+        pltpu.VMEM((LB // LANES, n_tok + HALO, LANES), F32),
+        pltpu.VMEM((n_tok, LB), F32),
         pltpu.VMEM((n_tok, LB), BF16),
         pltpu.VMEM((4, HALF, 3 * CHUNK), BF16),
         pltpu.VMEM((nb, state_dim, LB), F32),

time: 103 us -> 99.7 us (0.968)
  Pallas kernels: 98.2 us -> 95.4 us
    pallas_call x1, Pallas kernels: 98.2 us -> 95.4 us  [mixer(): pl.pallas_call(functools.partial(mixer_kernel, dims), out_shape=jax.Shape...]
where the time goes in v4:
time: 99.7 us; the launch traced here: 98.8 us
  Pallas kernels  95.4 us (96%)
  local copies, waits for them, and re-layouts  3.4 us (3%)
    pallas_call x1, Pallas kernels, mixer(): pl.pallas_call(functools.partial(mixer_kernel, dims), out_shape=jax.Shape...  95.4 us
    unnamed x1, local copies, waits for them, and re-layouts  3.4 us

profile of v4, /device:TPU:97, one launch (start us, length us, event | category | flops | bytes accessed | tf_op | source)
XLA Modules:
  0.0 98.8 jit_solution(7442105714863912554)
XLA Ops:
  0.0 95.4 %mixer.1 = bf16[512,2560]{1,0:T(8,128)(2,1)} custom-call(bf16[512,2560]{1,0:T(8,128)(2,1)} %x_hbm.1, s32[4,128]{1,0:T(4,128)} %bitcast.8, bf16[10576,2560]{1,0:T(8,128)(2,1)} %bitcast.6, bf16[5120,2560]{1,0:T(8,128)(2,1)} %wo_hbm.1, f32[4,5376]{1,0:T(4,128)} %cw_ref.1, f32[42,128]{1,0:T(8,128)} %bitcast.7, f32[1,80]{1,0:T(1,128)} %bitcast.9, ...), custom_call_target="tpu_custom_call" | custom-call | tf_op jit(solution)/shard_map/mixer/pallas_call | solution.py:605
  95.4 3.4 %copy.12 = bf16[512,2560]{1,0:T(8,128)(2,1)} copy(bf16[512,2560]{1,0:T(8,128)(2,1)} %mixer.1) | data formatting | bytes 5242880

commit v5 on v4

--- a/solution.py
+++ b/solution.py
@@ -43,7 +43,7 @@
 
 def mixer_kernel(dims, x_hbm, ds_ref, w_hbm, wo_hbm, cw_ref, cb_ref, dtb_ref, alog_ref, dsk_ref, nw_ref, o_hbm,
                  xe, wbuf, wbcd, zb, xb, yb, us, us2, yst, sc, mix, cs0, tsend, two, tc, hrecv, hout, s0r, fbuf, soth,
-                 bc, bt, gm, a2, apt, ldt, we, ws, arl, prm, dec, dpair, dchip, dg, mk, ssq, hal,
+                 bc, bt, gm, a2, apt, ldt, we, ws, arl, arm, prm, dec, dpair, dchip, dg, dga, mk, ssq, hal,
                  xsem, wsem, bsem, hs_sem, hr_sem, dp_sem, dps_sem, dg_sem, dgs_sem,
                  ps_sem, pr_sem, s1_sem, r1_sem, s2_sem, r2_sem, fs_sem, fr_sem, gsem):
     n_seq, n_tok, d_model, d_inner, n_heads, state_dim = dims
@@ -274,117 +274,13 @@
         return jnp.where(low_r, jnp.broadcast_to(wv[:, 2 * lt:2 * lt + 1], (ROWS, LANES)),
                          jnp.broadcast_to(wv[:, 2 * lt + 1:2 * lt + 2], (ROWS, LANES)))
 
-    def ublock(t_next, u_next, u_ref, b, t_ref):
-        wnext(t_next)
-        slot = lax.rem(t_next, 3)
-        roll_to(arl, we, b)
-        udot(slot, u_next)
-        for r0 in range(0, n_tok, ROWS):
-            for lt in range(n_lt):
-                cols = slice(lt * LANES, (lt + 1) * LANES)
-                xs = conv(u_ref, r0, lt, b * LB + lt * LANES).astype(BF16)
-                xb[b, r0:r0 + ROWS, cols] = xs
-                sc[r0:r0 + ROWS, cols] = (xs.astype(F32) * head_cols(r0, lt)).astype(BF16)
-
-        ex = expand(dec[...], b)
-        st0 = dot(bt[0], sc[0:CHUNK])
-        cs0[b] = st0
-        t_ref[...] = ex[1:2] * st0 + dot(bt[1], sc[CHUNK:2 * CHUNK])
-
-    def part_copy(i):
-        return pltpu.make_async_remote_copy(
-            src_ref=tsend.at[i], dst_ref=two.at[i, core], send_sem=ps_sem.at[i], recv_sem=pr_sem.at[i],
-            device_id=dev(partner), device_id_type=MESH)
-
-    def home_copy(i, q):
-        return pltpu.make_async_remote_copy(
-            src_ref=tc.at[i, q], dst_ref=hrecv.at[i, chip], send_sem=s1_sem.at[i], recv_sem=r1_sem.at[i],
-            device_id=dev(2 * q + core), device_id_type=MESH)
-
-    def back_copy(i, q):
-        return pltpu.make_async_remote_copy(
-            src_ref=hout.at[i, q], dst_ref=s0r.at[i, chip], send_sem=s2_sem.at[i], recv_sem=r2_sem.at[i],
-            device_id=dev(2 * q + core), device_id_type=MESH)
-
-    def all_copies(src, dst, send_sem, recv_sem):
-        return pltpu.make_async_remote_copy(
-            src_ref=src.at[pl.ds(0, n_chip - 1)], dst_ref=dst.at[pl.ds(0, n_chip - 1)], send_sem=send_sem, recv_sem=recv_sem,
-            device_id=dev(partner), device_id_type=MESH)
-
-    def fin_copy(i):
-        return pltpu.make_async_remote_copy(
-            src_ref=fbuf.at[i, 1 - core], dst_ref=soth.at[i], send_sem=fs_sem.at[i], recv_sem=fr_sem.at[i],
-            device_id=dev(partner), device_id_type=MESH)
-
-    def send_home(i, b):
-        part_copy(i).wait_recv()
-        ex = expand(dec[...], b)
-        for q in range(n_chip):
-            rows = slice(q * hrows, (q + 1) * hrows)
-            tc[i, q] = ex[3:4] * two[i, 0, rows] + two[i, 1, rows]
-        hrecv[i, chip] = tc[i, chip]
-
-        @pl.loop(1, n_chip, unroll=True)
-        def _(r):
-            home_copy(i, lax.rem(chip + r, n_chip)).start()
-
-    def home(i):
-        b = 2 * i + core
-        all_copies(tc.at[i], hrecv.at[i], s1_sem.at[i], r1_sem.at[i]).wait_recv()
-        run = jnp.zeros((hrows, LB), F32)
-        for q in range(n_chip):
-            hout[i, q] = run
-            run = expand(dg[q], b)[0:1] * run + hrecv[i, q]
-        s0r[i, chip] = hout[i, chip]
-
-        @pl.loop(1, n_chip, unroll=True)
-        def _(r):
-            back_copy(i, lax.rem(chip + r, n_chip)).start()
-
-    def finish(i):
-        b = 2 * i + core
-        all_copies(hout.at[i], s0r.at[i], s2_sem.at[i], r2_sem.at[i]).wait_recv()
-        ex = expand(dec[...], b)
-        for q in range(n_chip):
-            rows = slice(q * hrows, (q + 1) * hrows)
-            fbuf[i, 0, rows] = s0r[i, q]
-            fbuf[i, 1, rows] = ex[2:3] * s0r[i, q] + two[i, 0, rows]
-        fin_copy(i).start()
-
-    @pl.loop(0, npair)
-    def _(i):
-        t = n_zfirst + 2 * i
-        ublock(t + 1, us2, us, 2 * i + 1 - core, tsend.at[i])
-        part_copy(i).start()
-
-        @pl.when(i == 0)
-        def _():
-            send_decays()
-
-        ublock(t + 2, us, us2, 2 * i + core, two.at[i, core])
-        send_home(i, 2 * i + core)
-
-        @pl.when(i == 0)
-        def _():
-            all_copies(dg, dg, dgs_sem, dg_sem).wait_recv()
-
-        @pl.when(i >= 1)
-        def _():
-            home(i - 1)
-
-        @pl.when(i >= 3)
-        def _():
-            finish(i - 3)
-
-    for lt in range(n_lt):
-        zb[n_zfirst, :, lt * LANES:(lt + 1) * LANES] = us[lt, HALO:HALO + n_tok, :].astype(BF16)
-
     low_b = (lax.broadcasted_iota(jnp.int32, (CHUNK, LANES), 1) < head_dim).astype(F32).astype(BF16)
     high_b = (lax.broadcasted_iota(jnp.int32, (CHUNK, LANES), 1) >= head_dim).astype(F32).astype(BF16)
 
     sub = 32
 
     def intra(b):
+        roll_to(arm, a2, b)
         heads = pl.ds(pl.multiple_of(b * hb, hb), hb)
         dsk = expand(prm[...], b)[2:3]
         for c in range(n_chunks):
@@ -403,8 +299,8 @@
                         rr = slice(q * sub, (q + 1) * sub)
                         g0 = slice(q * sub, (q + 1) * sub)
                         g1 = slice(HALF + q * sub, HALF + (q + 1) * sub)
-                        ai0 = jnp.broadcast_to(arl[r0 + q * sub:r0 + (q + 1) * sub, h:h + 1], (sub, HALF))
-                        ai1 = jnp.broadcast_to(arl[r0 + HALF + q * sub:r0 + HALF + (q + 1) * sub, h:h + 1], (sub, HALF))
+                        ai0 = jnp.broadcast_to(arm[r0 + q * sub:r0 + (q + 1) * sub, h:h + 1], (sub, HALF))
+                        ai1 = jnp.broadcast_to(arm[r0 + HALF + q * sub:r0 + HALF + (q + 1) * sub, h:h + 1], (sub, HALF))
                         mix[k, rr, hh * HALF:(hh + 1) * HALF] = (jnp.exp2(jnp.minimum(ai0 - aj0, ld0)) * gm[c, g0, 0:HALF]).astype(BF16)
                         mix[k, rr, base:base + HALF] = (jnp.exp2(ai1 - aj0) * gm[c, g1, 0:HALF]).astype(BF16)
                         mix[k, rr, base + HALF:base + CHUNK] = (jnp.exp2(jnp.minimum(ai1 - aj1, ld1)) * gm[c, g1, HALF:CHUNK]).astype(BF16)
@@ -415,6 +311,115 @@
                 yb[b, r0:r0 + HALF, cols] = y0 + dsk[:, cols] * xp[:HALF].astype(F32)
                 yb[b, r0 + HALF:r0 + CHUNK, cols] = y1 + dsk[:, cols] * xp[HALF:].astype(F32)
 
+    def ublock(t_next, u_next, u_ref, b, t_ref, b_done):
+        wnext(t_next)
+        slot = lax.rem(t_next, 3)
+        roll_to(arl, we, b)
+        udot(slot, u_next)
+        for r0 in range(0, n_tok, ROWS):
+            for lt in range(n_lt):
+                cols = slice(lt * LANES, (lt + 1) * LANES)
+                xs = conv(u_ref, r0, lt, b * LB + lt * LANES).astype(BF16)
+                xb[b, r0:r0 + ROWS, cols] = xs
+                sc[r0:r0 + ROWS, cols] = (xs.astype(F32) * head_cols(r0, lt)).astype(BF16)
+
+        intra(b_done)
+        ex = expand(dec[...], b)
+        st0 = dot(bt[0], sc[0:CHUNK])
+        cs0[b] = st0
+        t_ref[...] = ex[1:2] * st0 + dot(bt[1], sc[CHUNK:2 * CHUNK])
+
+    def part_copy(i):
+        return pltpu.make_async_remote_copy(
+            src_ref=tsend.at[i], dst_ref=two.at[i, core], send_sem=ps_sem.at[i], recv_sem=pr_sem.at[i],
+            device_id=dev(partner), device_id_type=MESH)
+
+    def home_copy(i, q):
+        return pltpu.make_async_remote_copy(
+            src_ref=tc.at[i, q], dst_ref=hrecv.at[i, chip], send_sem=s1_sem.at[i], recv_sem=r1_sem.at[i],
+            device_id=dev(2 * q + core), device_id_type=MESH)
+
+    def back_copy(i, q):
+        return pltpu.make_async_remote_copy(
+            src_ref=hout.at[i, q], dst_ref=s0r.at[i, chip], send_sem=s2_sem.at[i], recv_sem=r2_sem.at[i],
+            device_id=dev(2 * q + core), device_id_type=MESH)
+
+    def all_copies(src, dst, send_sem, recv_sem):
+        return pltpu.make_async_remote_copy(
+            src_ref=src.at[pl.ds(0, n_chip - 1)], dst_ref=dst.at[pl.ds(0, n_chip - 1)], send_sem=send_sem, recv_sem=recv_sem,
+            device_id=dev(partner), device_id_type=MESH)
+
+    def fin_copy(i):
+        return pltpu.make_async_remote_copy(
+            src_ref=fbuf.at[i, 1 - core], dst_ref=soth.at[i], send_sem=fs_sem.at[i], recv_sem=fr_sem.at[i],
+            device_id=dev(partner), device_id_type=MESH)
+
+    def send_home(i, b):
+        part_copy(i).wait_recv()
+        ex = expand(dec[...], b)
+        for q in range(n_chip):
+            rows = slice(q * hrows, (q + 1) * hrows)
+            tc[i, q] = ex[3:4] * two[i, 0, rows] + two[i, 1, rows]
+        hrecv[i, chip] = tc[i, chip]
+
+        @pl.loop(1, n_chip, unroll=True)
+        def _(r):
+            home_copy(i, lax.rem(chip + r, n_chip)).start()
+
+    def home(i):
+        b = 2 * i + core
+        all_copies(tc.at[i], hrecv.at[i], s1_sem.at[i], r1_sem.at[i]).wait_recv()
+        ex = expand(dga[...], b)
+        run = jnp.zeros((hrows, LB), F32)
+        for q in range(n_chip):
+            hout[i, q] = run
+            run = ex[q:q + 1] * run + hrecv[i, q]
+        s0r[i, chip] = hout[i, chip]
+
+        @pl.loop(1, n_chip, unroll=True)
+        def _(r):
+            back_copy(i, lax.rem(chip + r, n_chip)).start()
+
+    def finish(i):
+        b = 2 * i + core
+        all_copies(hout.at[i], s0r.at[i], s2_sem.at[i], r2_sem.at[i]).wait_recv()
+        ex = expand(dec[...], b)
+        for q in range(n_chip):
+            rows = slice(q * hrows, (q + 1) * hrows)
+            fbuf[i, 0, rows] = s0r[i, q]
+            fbuf[i, 1, rows] = ex[2:3] * s0r[i, q] + two[i, 0, rows]
+        fin_copy(i).start()
+
+    @pl.loop(0, npair)
+    def _(i):
+        t = n_zfirst + 2 * i
+        ublock(t + 1, us2, us, 2 * i + 1 - core, tsend.at[i], 2 * jnp.maximum(i - 1, 0) + core)
+        part_copy(i).start()
+
+        @pl.when(i == 0)
+        def _():
+            send_decays()
+
+        ublock(t + 2, us, us2, 2 * i + core, two.at[i, core], 2 * i + 1 - core)
+        send_home(i, 2 * i + core)
+
+        @pl.when(i == 0)
+        def _():
+            all_copies(dg, dg, dgs_sem, dg_sem).wait_recv()
+            for q in range(n_chip):
+                dga[q:q + 1, :] = dg[q, 0:1, :]
+
+        @pl.when(i >= 1)
+        def _():
+            home(i - 1)
+
+        @pl.when(i >= 3)
+        def _():
+            finish(i - 3)
+
+    for lt in range(n_lt):
+        zb[n_zfirst, :, lt * LANES:(lt + 1) * LANES] = us[lt, HALO:HALO + n_tok, :].astype(BF16)
+
     def zdot(t, zi):
         slot = lax.rem(t, 3)
         zb[zi] = dot_nt(xe[HALO:HALO + n_tok], wbuf[slot]).astype(BF16)
@@ -423,26 +428,19 @@
     def _(m):
         t = t_z + 1 + m
         wnext(t)
-        roll_to(arl, a2, m)
         zdot(t, n_zfirst + 2 * (m + 1))
-        intra(m)
 
         @pl.when(m == 0)
         def _():
             finish(npair - 3)
 
+        @pl.when(m == 1)
+        def _():
+            intra(2 * (npair - 1) + core)
+
         @pl.when(m == n_zmid - 1)
         def _():
             home(npair - 1)
-
-    @pl.loop(n_zmid, nb)
-    def _(m):
-        roll_to(arl, a2, m)
-        intra(m)
-
-        @pl.when(m == nb - 4)
-        def _():
-            finish(npair - 2)
 
     ssq[...] = jnp.zeros((n_tok, LANES), F32)
 
@@ -479,6 +477,10 @@
         close(2 * i + core, fbuf.at[i, core])
         close(2 * i + 1 - core, soth.at[i])
 
+        @pl.when(i == 0)
+        def _():
+            finish(npair - 2)
+
         @pl.when(i == npair - 3)
         def _():
             finish(npair - 1)
@@ -502,6 +504,9 @@
     def _(b):
         normalize(b)
 
+    def ocopy(n):
+        return pltpu.make_async_copy(xb.at[n], o_hbm.at[:, n * LB:(n + 1) * LB], gsem.at[n])
+
     def project(b, first, last):
         wnext(b + 2 * nb)
         slot = lax.rem(b + 2 * nb, 3)
@@ -511,11 +516,9 @@
                 part = yb[n] + part
             if last:
                 xb[n] = part.astype(BF16)
+                ocopy(n).start()
             else:
                 yb[n] = part
-
-    def ocopy(n):
-        return pltpu.make_async_copy(xb.at[n], o_hbm.at[:, n * LB:(n + 1) * LB], gsem.at[n])
 
     project(jnp.int32(0), True, False)
 
@@ -527,8 +530,6 @@
         project(b, False, False)
 
     project(jnp.int32(nb - 1), False, True)
-    for n in range(n_out):
-        ocopy(n).start()
 
     @pl.when(me < n_seq - 1)
     def _():
@@ -590,11 +591,13 @@
         pltpu.VMEM((n_tok, LANES), F32),
         pltpu.VMEM((n_tok, LANES), F32),
         pltpu.VMEM((n_tok, LANES), F32),
+        pltpu.VMEM((n_tok, LANES), F32),
         pltpu.VMEM((8, LANES), F32),
         pltpu.VMEM((8, LANES), F32),
         pltpu.VMEM((2, 8, LANES), F32),
         pltpu.VMEM((8, LANES), F32),
         pltpu.VMEM((n_chip, 8, LANES), F32),
+        pltpu.VMEM((n_chip, LANES), F32),
         pltpu.VMEM((3, n_tok, LANES), F32),
         pltpu.VMEM((n_tok, LANES), F32),
         pltpu.VMEM((HALO, d_model), BF16),

time: 99.7 us -> 90.3 us (0.906)
  Pallas kernels: 95.4 us -> 86.8 us
    pallas_call x1, Pallas kernels: 95.4 us -> 86.8 us  [mixer(): pl.pallas_call(functools.partial(mixer_kernel, dims), out_shape=jax.Shape...]
where the time goes in v5:
time: 90.3 us; the launch traced here: 90.2 us
  Pallas kernels  86.8 us (96%)
  local copies, waits for them, and re-layouts  3.4 us (4%)
    pallas_call x1, Pallas kernels, mixer(): pl.pallas_call(functools.partial(mixer_kernel, dims), out_shape=jax.Shape...  86.8 us
    unnamed x1, local copies, waits for them, and re-layouts  3.4 us

profile of v5, /device:TPU:97, one launch (start us, length us, event | category | flops | bytes accessed | tf_op | source)
XLA Modules:
  0.0 90.2 jit_solution(3923110501282944626)
XLA Ops:
  0.0 86.8 %mixer.1 = bf16[512,2560]{1,0:T(8,128)(2,1)} custom-call(bf16[512,2560]{1,0:T(8,128)(2,1)} %x_hbm.1, s32[4,128]{1,0:T(4,128)} %bitcast.8, bf16[10576,2560]{1,0:T(8,128)(2,1)} %bitcast.6, bf16[5120,2560]{1,0:T(8,128)(2,1)} %wo_hbm.1, f32[4,5376]{1,0:T(4,128)} %cw_ref.1, f32[42,128]{1,0:T(8,128)} %bitcast.7, f32[1,80]{1,0:T(1,128)} %bitcast.9, ...), custom_call_target="tpu_custom_call" | custom-call | tf_op jit(solution)/shard_map/mixer/pallas_call | solution.py:608
  86.8 3.4 %copy.12 = bf16[512,2560]{1,0:T(8,128)(2,1)} copy(bf16[512,2560]{1,0:T(8,128)(2,1)} %mixer.1) | data formatting | bytes 5242880

commit v6 on v5

--- a/solution.py
+++ b/solution.py
@@ -101,9 +101,7 @@
     xcopy.start()
     wcopy(jnp.int32(0)).start()
     bcopy = pltpu.make_async_copy(w_hbm.at[pl.ds(2 * d_inner, n_bcd)], wbcd.at[pl.ds(0, n_bcd)], bsem)
-    bcopy.start()
     wbcd[n_bcd:, :] = jnp.zeros((LANES - n_heads, d_model), BF16)
-    wcopy(jnp.int32(1)).start()
 
     barrier = pltpu.get_barrier_semaphore()
     pl.semaphore_signal(barrier, inc=1, device_id=dev(lax.rem(me + 1, n_seq)), device_id_type=MESH)
@@ -136,6 +134,8 @@
     mk[2] = m1 * k1 * k2
 
     xcopy.wait()
+    wcopy(jnp.int32(1)).start()
+    bcopy.start()
     hrow = lax.broadcasted_iota(jnp.int32, (HALO, LANES), 0)
     k_last = jnp.broadcast_to(mk[0, n_tok - 8:n_tok, :][7:8, :], (HALO, LANES))
     k_last2 = jnp.broadcast_to(mk[1, n_tok - 8:n_tok, :][7:8, :], (HALO, LANES))

time: 90.3 us -> 90.8 us (level)
  no operation moved by 1% of the time
where the time goes in v6:
time: 90.8 us; the launch traced here: 90.6 us
  Pallas kernels  87.2 us (96%)
  local copies, waits for them, and re-layouts  3.4 us (4%)
    pallas_call x1, Pallas kernels, mixer(): pl.pallas_call(functools.partial(mixer_kernel, dims), out_shape=jax.Shape...  87.2 us
    unnamed x1, local copies, waits for them, and re-layouts  3.4 us

profile of v6, /device:TPU:97, one launch (start us, length us, event | category | flops | bytes accessed | tf_op | source)
XLA Modules:
  0.0 90.6 jit_solution(9315672562760743959)
XLA Ops:
  0.0 87.2 %mixer.1 = bf16[512,2560]{1,0:T(8,128)(2,1)} custom-call(bf16[512,2560]{1,0:T(8,128)(2,1)} %x_hbm.1, s32[4,128]{1,0:T(4,128)} %bitcast.8, bf16[10576,2560]{1,0:T(8,128)(2,1)} %bitcast.6, bf16[5120,2560]{1,0:T(8,128)(2,1)} %wo_hbm.1, f32[4,5376]{1,0:T(4,128)} %cw_ref.1, f32[42,128]{1,0:T(8,128)} %bitcast.7, f32[1,80]{1,0:T(1,128)} %bitcast.9, ...), custom_call_target="tpu_custom_call" | custom-call | tf_op jit(solution)/shard_map/mixer/pallas_call | solution.py:608
  87.2 3.4 %copy.12 = bf16[512,2560]{1,0:T(8,128)(2,1)} copy(bf16[512,2560]{1,0:T(8,128)(2,1)} %mixer.1) | data formatting | bytes 5242880
